TPU v7x, 128 devices: a whole 4x4x4 slice. The times are simulated.
128 devices in a mesh: dp: 8 (over z, core), mp: 16 (over y, x).
Axes of the slice: x: 4, y: 4, z: 4, core: 2. Of those that a mesh axis runs over, the one named last changes fastest.
Arguments:
- patches: bfloat16 [16384, 1280], P(('dp', 'mp')), may hold values from -6 to 6
- window_ids: int32 [128, 128], P(('dp', 'mp')), may hold values from 0 to 7, never falling along the last dimension, each value on 1 to 64 neighbouring positions
- owner: int32 [4096, 1], P(('dp', 'mp')), may hold values from 0 to 7; in each aligned block of 32 rows (0 to 31, 32 to 63, ...) at most 8 rows name the same one
- slot_of_row: int32 [128, 64], P(('dp', 'mp')), may hold values from 0 to 63, each once within a row
- text_embeds: bfloat16 [8192, 8192], P(('dp', 'mp')), may hold values from -6 to 6
- vit_norm: float32 [1280], replicated, may hold values from 0.3 to 3
- vit_qkv_w: bfloat16 [1280, 1920], replicated, may hold values from -0.15625 to 0.15625
- vit_qkv_b: float32 [1920], replicated, may hold values from -12 to 12
- vit_out_w: bfloat16 [640, 1280], replicated, may hold values from -0.25 to 0.25
- merge_norm: float32 [1280], replicated, may hold values from 0.3 to 3
- merge_w1: bfloat16 [5120, 5120], P(None, 'mp'), may hold values from -0.078125 to 0.078125
- merge_b1: float32 [5120], P('mp'), may hold values from -3 to 3
- merge_w2: bfloat16 [5120, 8192], P('mp'), may hold values from -0.078125 to 0.078125
- merge_b2: float32 [8192], replicated, may hold values from -3 to 3
- llm_norm: float32 [8192], replicated, may hold values from 0.5 to 1.5
- q_w: bfloat16 [8192, 4096], P(None, 'mp'), may hold values from -0.0625 to 0.0625
- q_b: float32 [4096], P('mp'), may hold values from -12 to 12
- kv_w: bfloat16 [2, 8192, 512], P(None, None, 'mp'), may hold values from -0.0625 to 0.0625
- kv_b: float32 [2, 512], P(None, 'mp'), may hold values from -12 to 12
Outputs:
- attended: bfloat16 [8192, 4096], P('dp', 'mp')
Inputs may be any that keep to these rules, and one draw needn't show every extreme that they name: `window_ids`: within each block, window numbers never fall and each window has at most 64 patches. Among the 32 merged rows of one device, no owner is named by more than 8 rows, a bound that some block reaches. `slot_of_row`: each row is a permutation of the 64 slots.
All inputs are finite; a program needn't handle non-finite values.
Results may differ from a plain program's by a relative error of at most 0.04.
Values may be sent and summed in bfloat16 or wider, within the bound.
A program may use at most 128 MiB of HBM per device.

v0:
```python
import jax
import jax.numpy as jnp
from jax import lax
from jax.sharding import PartitionSpec as P

VHD = 80
HD = 128
QH = 32
KVH = 4


epsilon = 1e-06


def laid_out(parts, dim):
    lengths = list(parts.shape[1:])
    lengths[dim] *= parts.shape[0]
    return jnp.moveaxis(parts, 0, dim).reshape(lengths)


def copy_for_each(x, axis):
    size = lax.axis_size(axis)
    return lax.all_to_all(jnp.broadcast_to(x[None], (size, *x.shape)), axis, 0, 0, tiled=True)


def gathered_copies(x, axis, dim):
    return laid_out(copy_for_each(x, axis), dim)


def rms_norm(inputs, gain):
    inputs = inputs.astype(jnp.float32)
    return inputs * lax.rsqrt(jnp.mean(inputs * inputs, axis=-1, keepdims=True) + epsilon) * gain


def vision_block(patches, window_ids, vit_norm, vit_qkv_w, vit_qkv_b, vit_out_w, merge_norm):
    normed = rms_norm(patches, vit_norm).astype(jnp.bfloat16)
    projected = (jnp.dot(normed, vit_qkv_w, preferred_element_type=jnp.float32) + vit_qkv_b).astype(
        jnp.bfloat16
    )
    blocks = window_ids.shape[0]
    width = window_ids.shape[1]
    inner_width = vit_out_w.shape[0]
    heads = inner_width // VHD
    shaped = projected.reshape(blocks, width, 3, heads, VHD)
    scores = jnp.einsum(
        "bqhd,bkhd->bhqk", shaped[:, :, 0], shaped[:, :, 1], preferred_element_type=jnp.float32
    ) * VHD ** (-0.5)
    in_window = window_ids[:, None, :, None] == window_ids[:, None, None, :]
    scores = jnp.where(in_window, scores, -1e30)
    peak = jnp.max(scores, axis=-1, keepdims=True)
    weights = jnp.exp(scores - peak)
    weights = (weights / jnp.sum(weights, axis=-1, keepdims=True)).astype(jnp.bfloat16)
    mixture = jnp.einsum(
        "bhqk,bkhd->bqhd", weights, shaped[:, :, 2], preferred_element_type=jnp.float32
    )
    mixture = mixture.astype(jnp.bfloat16).reshape(blocks * width, inner_width)
    residual = (
        patches.astype(jnp.float32)
        + jnp.dot(mixture, vit_out_w, preferred_element_type=jnp.float32)
    ).astype(jnp.bfloat16)
    merged = rms_norm(residual, merge_norm).astype(jnp.bfloat16)
    return merged.reshape(blocks * width // 4, 4 * patches.shape[1])


def shards(
    patches,
    window_ids,
    owner,
    slot_of_row,
    text_embeds,
    vit_norm,
    vit_qkv_w,
    vit_qkv_b,
    vit_out_w,
    merge_norm,
    merge_w1,
    merge_b1,
    merge_w2,
    merge_b2,
    llm_norm,
    q_w,
    q_b,
    kv_w,
    kv_b,
):
    merged = vision_block(
        patches, window_ids, vit_norm, vit_qkv_w, vit_qkv_b, vit_out_w, merge_norm
    )
    own_index = lax.axis_index("mp")
    rows_all = lax.all_gather(merged, "mp", axis=0, tiled=True)
    hidden = jax.nn.gelu(
        jnp.dot(rows_all, merge_w1, preferred_element_type=jnp.float32) + merge_b1,
        approximate=False,
    ).astype(jnp.bfloat16)
    own_rows = lax.psum_scatter(
        jnp.dot(hidden, merge_w2, preferred_element_type=jnp.float32).astype(jnp.bfloat16),
        "mp",
        scatter_dimension=0,
        tiled=True,
    ).astype(jnp.float32)
    embedded = (own_rows + merge_b2).astype(jnp.bfloat16)
    seq_rows = text_embeds.shape[0]
    groups = lax.axis_size("dp")
    capacity = seq_rows // groups
    target_group = owner[:, 0]
    onehot = (target_group[:, None] == jnp.arange(groups, dtype=jnp.int32)[None, :]).astype(
        jnp.int32
    )
    rank_in = jnp.sum((jnp.cumsum(onehot, axis=0) - onehot) * onehot, axis=1)
    send_slot = target_group * capacity + rank_in
    selector = send_slot[None, :] == jnp.arange(seq_rows, dtype=jnp.int32)[:, None]
    buffer = jnp.dot(
        selector.astype(jnp.bfloat16), embedded, preferred_element_type=jnp.float32
    ).astype(jnp.bfloat16)
    buffer = buffer.reshape(groups, capacity, embedded.shape[1])
    marks = jnp.sum(selector.astype(jnp.int32), axis=1).reshape(groups, capacity)
    arrived, arrived_marks = (
        lax.all_to_all(buffer, "dp", split_axis=0, concat_axis=0, tiled=True),
        lax.all_to_all(marks, "dp", split_axis=0, concat_axis=0, tiled=True),
    )
    arrived = arrived.reshape(seq_rows, embedded.shape[1])
    arrived_marks = arrived_marks.reshape(seq_rows)
    chosen = slot_of_row[0]
    sequence = jnp.where(arrived_marks[chosen][:, None] > 0, arrived[chosen], text_embeds)
    llm_normed = rms_norm(sequence, llm_norm).astype(jnp.bfloat16)
    query_cols = q_w.shape[1]
    kv_cols = kv_w.shape[2]
    shard_rows = lax.all_gather(llm_normed, "mp", axis=0, tiled=True)
    projected = jnp.concatenate(
        [
            jnp.dot(shard_rows, q_w, preferred_element_type=jnp.float32),
            jnp.dot(shard_rows, kv_w[0], preferred_element_type=jnp.float32),
            jnp.dot(shard_rows, kv_w[1], preferred_element_type=jnp.float32),
        ],
        axis=1,
    )
    length = projected.shape[0]
    queries = (projected[:, :query_cols] + q_b).astype(jnp.bfloat16)
    key_rows = (projected[:, query_cols : query_cols + kv_cols] + kv_b[0]).astype(jnp.bfloat16)
    value_rows = (projected[:, query_cols + kv_cols :] + kv_b[1]).astype(jnp.bfloat16)
    stacked = jnp.stack([key_rows.T, value_rows.T])
    all_heads = gathered_copies(stacked, "mp", 1)
    heads_here = query_cols // HD
    group_size = QH // KVH
    kv_head = own_index * heads_here // group_size
    by_head = all_heads.reshape(2, HD, KVH, length)
    key_cols = lax.dynamic_index_in_dim(by_head[0], kv_head, 1, keepdims=False)
    value_cols = lax.dynamic_index_in_dim(by_head[1], kv_head, 1, keepdims=False)
    query_heads = queries.reshape(length, heads_here, HD)
    scores = jnp.einsum(
        "qhd,dk->hqk", query_heads, key_cols, preferred_element_type=jnp.float32
    ) * HD ** (-0.5)
    allowed = jnp.arange(length)[:, None] >= jnp.arange(length)[None, :]
    scores = jnp.where(allowed[None], scores, -1e30)
    peak = jnp.max(scores, axis=-1, keepdims=True)
    weights = jnp.exp(scores - peak)
    weights = (weights / jnp.sum(weights, axis=-1, keepdims=True)).astype(jnp.bfloat16)
    mixture = jnp.einsum("hqk,dk->qhd", weights, value_cols, preferred_element_type=jnp.float32)
    return mixture.astype(jnp.bfloat16).reshape(length, query_cols)


def solution(mesh):
    return jax.shard_map(
        shards,
        mesh=mesh,
        in_specs=(
            P(("dp", "mp"), None),
            P(("dp", "mp"), None),
            P(("dp", "mp"), None),
            P(("dp", "mp"), None),
            P(("dp", "mp"), None),
            P(),
            P(),
            P(),
            P(),
            P(),
            P(None, "mp"),
            P("mp"),
            P("mp", None),
            P(),
            P(),
            P(None, "mp"),
            P("mp"),
            P(None, None, "mp"),
            P(None, "mp"),
        ),
        out_specs=P("dp", "mp"),
        check_vma=False,
    )
```

profile of v0, /device:TPU:0, one launch (start us, length us, event | category | flops | bytes accessed | tf_op | source)
XLA Modules:
  0.0 402.4 jit_solution(15220331925522827266)
XLA Ops:
  6.5 0.9 broadcast_compare_fusion
  7.5 1.2 fusion.25
  8.7 4.3 %fusion.10 = bf16[128,1920]{1,0:T(8,128)(2,1)} fusion(bf16[1280,1920]{1,0:T(8,128)(2,1)} %param.25, f32[1920]{0:T(1024)} %param.26, bf16[128,1280]{1,0:T(8,128)(2,1)} %param.19, f32[1280]{0:T(1024)} %param.24, f32[128]{0:T(128)S(1)} %add_rsqrt_fusion.2), kind=kOutput, calls=%fused_computation.22 | convolution fusion | flops 630292480 | bytes 5747712 | tf_op jit(solution)/shard_map/dot_general | solution.py:37
  12.9 2.0 copy.47
  15.0 1.4 fusion.119
  16.3 2.1 fusion.18
  18.4 1.5 convolution_convert_fusion.2
  19.9 2.0 multiply_reduce_fusion
  22.8 1.9 reshape.196
  24.8 58.6 %all-gather.3.cloned.1.call-done = bf16[512,5120]{1,0:T(8,128)(2,1)} async-done(((bf16[32,5120]{1,0:T(8,128)(2,1)}), bf16[512,5120]{1,0:T(8,128)(2,1)}) %all-gather.3.cloned.1.call-update) | async-done | bytes 5242896 | tf_op jit(solution)/shard_map/all_gather | solution.py:90
  83.4 16.7 %convolution_convert_fusion = bf16[512,8192]{1,0:T(8,128)(2,1)} fusion(bf16[320,8192]{1,0:T(8,128)(2,1)} %param.31, bf16[512,5120]{1,0:T(8,128)(2,1)} %all-gather.3.cloned.1.call-done, bf16[5120,320]{0,1:T(8,128)(2,1)S(1)} %copy-done, f32[320]{0:T(512)S(1)} %copy-done.10), kind=kOutput, calls=%fused_computation.4 | convolution fusion | flops 4377083904 | bytes 22152448 | tf_op jit(solution)/shard_map/dot_general | solution.py:96
  101.8 4.4 %all-to-all-start = ((s32[8,1,8]{2,1,0:T(1,128)}), s32[8,1,8]{2,1,0:T(1,128)S(1)}, u32[]{:S(2)}, u32[]{:S(2)}) async-start(s32[8,1,8]{2,1,0:T(1,128)} %bitcast.1), calls=%async_computation | async-start | bytes 8192 | tf_op jit(solution)/shard_map/all_to_all | solution.py:119
  106.2 79.8 %reduce-scatter.2.cloned.1.call-done = bf16[32,8192]{1,0:T(8,128)(2,1)} async-done(((bf16[512,8192]{1,0:T(8,128)(2,1)}), bf16[32,8192]{1,0:T(8,128)(2,1)}) %reduce-scatter.2.cloned.1.call-update) | async-done | bytes 524304 | tf_op jit(solution)/shard_map/reduce_scatter | solution.py:95
  186.0 2.6 fusion.2
  188.6 4.4 %all-to-all-start.1 = ((bf16[8,8,8192]{2,1,0:T(8,128)(2,1)}), bf16[8,8,8192]{2,1,0:T(8,128)(2,1)S(1)}, u32[]{:S(2)}, u32[]{:S(2)}) async-start(bf16[8,8,8192]{2,1,0:T(8,128)(2,1)} %fusion.2), calls=%async_computation.2 | async-start | bytes 2097152 | tf_op jit(solution)/shard_map/all_to_all | solution.py:118
  195.4 13.6 %all-to-all-done.1 = bf16[8,8,8192]{2,1,0:T(8,128)(2,1)S(1)} async-done(((bf16[8,8,8192]{2,1,0:T(8,128)(2,1)}), bf16[8,8,8192]{2,1,0:T(8,128)(2,1)S(1)}, u32[]{:S(2)}, u32[]{:S(2)}) %all-to-all-start.1) | async-done | bytes 1048608 | tf_op jit(solution)/shard_map/all_to_all | solution.py:118
  209.0 1.2 gather_fusion.1
  210.8 1.5 fusion.13
  212.3 108.6 %all-gather.5.cloned.1.call-done = bf16[1024,8192]{1,0:T(8,128)(2,1)} async-done(((bf16[64,8192]{1,0:T(8,128)(2,1)}), bf16[1024,8192]{1,0:T(8,128)(2,1)}) %all-gather.5.cloned.1.call-update) | async-done | bytes 16777232 | tf_op jit(solution)/shard_map/all_gather | solution.py:128
  320.9 10.9 %fusion.21 = bf16[1,32,1024]{2,1,0:T(8,128)(2,1)S(1)} fusion(bf16[1024,8192]{1,0:T(8,128)(2,1)} %all-gather.5.cloned.1.call-done, bf16[2,8192,32]{1,2,0:T(8,128)(2,1)S(1)} %copy-done.4, f32[32]{0:T(128)S(1)} %get-tuple-element.8), kind=kOutput, calls=%fused_computation.39 | convolution fusion | flops 536936448 | bytes 17367552 | tf_op jit(solution)/shard_map/dot_general | solution.py:133
  331.8 5.0 %fusion.22 = bf16[1,32,1024]{2,1,0:T(8,128)(2,1)S(1)} fusion(bf16[1024,8192]{1,0:T(8,128)(2,1)S(1)} %copy-done.2, bf16[2,8192,32]{1,2,0:T(8,128)(2,1)S(1)} %copy-done.4, f32[32]{0:T(128)S(1)} %get-tuple-element.7), kind=kOutput, calls=%fused_computation.40 | convolution fusion | flops 536936448 | bytes 17367552 | tf_op jit(solution)/shard_map/dot_general | solution.py:132
  336.9 1.6 broadcast_in_dim.33
  338.5 5.3 %all-to-all-start.2 = ((bf16[16,2,32,1024]{3,2,1,0:T(8,128)(2,1)}), bf16[16,2,32,1024]{3,2,1,0:T(8,128)(2,1)S(1)}, u32[]{:S(2)}, u32[]{:S(2)}) async-start(bf16[16,2,32,1024]{3,2,1,0:T(8,128)(2,1)} %broadcast_in_dim.33), calls=%async_computation.3 | async-start | bytes 4194304 | tf_op jit(solution)/shard_map/all_to_all | solution.py:23
  343.8 1.3 iota_compare_fusion
  345.1 10.0 %fusion.14 = bf16[1024,256]{0,1:T(8,128)(2,1)} fusion(bf16[1024,8192]{1,0:T(8,128)(2,1)} %all-gather.5.cloned.1.call-done, bf16[8192,256]{1,0:T(8,128)(2,1)} %param.34, f32[256]{0:T(256)S(1)} %copy-done.11), kind=kOutput, calls=%fused_computation.27 | convolution fusion | flops 4295491584 | bytes 21496832 | tf_op jit(solution)/shard_map/dot_general | solution.py:131
  355.2 20.0 %all-to-all-done.2 = bf16[16,2,32,1024]{3,2,1,0:T(8,128)(2,1)S(1)} async-done(((bf16[16,2,32,1024]{3,2,1,0:T(8,128)(2,1)}), bf16[16,2,32,1024]{3,2,1,0:T(8,128)(2,1)S(1)}, u32[]{:S(2)}, u32[]{:S(2)}) %all-to-all-start.2) | async-done | bytes 2097184 | tf_op jit(solution)/shard_map/all_to_all | solution.py:23
  375.2 1.3 fusion.118
  376.4 1.5 squeeze.34
  378.3 1.9 constant_dynamic-slice_fusion
  380.7 7.8 %fusion.120 = (f32[2,1024]{1,0:T(2,128)S(1)}, f32[2,1024,1024]{1,2,0:T(8,128)}) fusion(pred[1024,1024]{0,1:T(8,128)(4,1)} %iota_compare_fusion, bf16[1024,2,128]{0,2,1:T(8,128)(2,1)} %bitcast.116, bf16[128,1,1024]{0,2,1:T(8,128)(2,1)S(1)} %copy.49), kind=kOutput, calls=%fused_computation.168 | convolution fusion | flops 545260544 | bytes 10231808 | tf_op jit(solution)/shard_map/sub | solution.py:156
  388.5 5.3 %fusion.15 = bf16[128,2,1024]{2,0,1:T(8,128)(2,1)} fusion(f32[2,1024,1024]{1,2,0:T(8,128)} %get-tuple-element.12, f32[2,1024]{1,0:T(2,128)S(1)} %get-tuple-element.11, bf16[128,1,1024]{2,1,0:T(2,128)(2,1)} %get-tuple-element.14), kind=kOutput, calls=%fused_computation.28 | convolution fusion | flops 541327360 | bytes 9183232 | tf_op jit(solution)/shard_map/hqk,dk->qhd/dot_general | solution.py:158
  393.8 2.0 copy.52
  (55 shorter events, 6.4 us)
Async XLA Ops:
  6.5 76.9 %copy-start = (bf16[5120,320]{0,1:T(8,128)(2,1)S(1)}, bf16[5120,320]{0,1:T(8,128)(2,1)}, u32[]{:S(2)}) copy-start(bf16[5120,320]{0,1:T(8,128)(2,1)} %param.29) | copy-start | bytes 9830404
  6.5 76.9 %all-gather.3.cloned.1.call-start = ((), (), s32[]{:S(2)}) async-start(), calls=%async_computation.4 | async-start | bytes 5570560 | tf_op jit(solution)/shard_map/all_gather | solution.py:90
  12.9 9.0 %copy-start.7 = (f32[1280]{0:T(1024)S(1)}, f32[1280]{0:T(1024)}, u32[]{:S(2)}) copy-start(f32[1280]{0:T(1024)} %param.28) | copy-start | bytes 15364
  12.9 70.5 %copy-start.10 = (f32[320]{0:T(512)S(1)}, f32[320]{0:T(512)}, u32[]{:S(2)}) copy-start(f32[320]{0:T(512)} %param.30) | copy-start | bytes 3844
  24.7 161.3 %reduce-scatter.2.cloned.1.call-start = ((), (), s32[]{:S(2)}) async-start(), calls=%async_computation.5 | async-start | bytes 8912896 | tf_op jit(solution)/shard_map/reduce_scatter | solution.py:95
  100.1 0.7 copy-start.8
  100.1 86.0 %copy-start.6 = (f32[8192]{0:T(1024)S(1)}, f32[8192]{0:T(1024)}, u32[]{:S(2)}) copy-start(f32[8192]{0:T(1024)} %param.32) | copy-start | bytes 98308
  100.1 93.2 %copy-start.12 = (s32[1,64]{1,0:T(1,128)S(1)}, s32[1,64]{1,0:T(1,128)}, u32[]{:S(2)}) copy-start(s32[1,64]{1,0:T(1,128)} %param.22) | copy-start | bytes 772
  101.8 86.8 %all-to-all-start = ((s32[8,1,8]{2,1,0:T(1,128)}), s32[8,1,8]{2,1,0:T(1,128)S(1)}, u32[]{:S(2)}, u32[]{:S(2)}) async-start(s32[8,1,8]{2,1,0:T(1,128)} %bitcast.1), calls=%async_computation | async-start | bytes 8192 | tf_op jit(solution)/shard_map/all_to_all | solution.py:119
  188.6 20.4 %all-to-all-start.1 = ((bf16[8,8,8192]{2,1,0:T(8,128)(2,1)}), bf16[8,8,8192]{2,1,0:T(8,128)(2,1)S(1)}, u32[]{:S(2)}, u32[]{:S(2)}) async-start(bf16[8,8,8192]{2,1,0:T(8,128)(2,1)} %fusion.2), calls=%async_computation.2 | async-start | bytes 2097152 | tf_op jit(solution)/shard_map/all_to_all | solution.py:118
  193.0 17.1 %copy-start.3 = (bf16[64,8192]{1,0:T(8,128)(2,1)S(1)}, bf16[64,8192]{1,0:T(8,128)(2,1)}, u32[]{:S(2)}) copy-start(bf16[64,8192]{1,0:T(8,128)(2,1)} %param.23) | copy-start | bytes 3145732
  193.0 127.8 %all-gather.5.cloned.1.call-start = ((), (), s32[]{:S(2)}) async-start(), calls=%async_computation.6 | async-start | bytes 17825792 | tf_op jit(solution)/shard_map/all_gather | solution.py:128
  209.0 1.8 copy-start.5
  210.2 2.1 copy-start.9
  210.2 110.7 %copy-start.4 = (bf16[2,8192,32]{1,2,0:T(8,128)(2,1)S(1)}, bf16[2,8192,32]{1,2,0:T(8,128)(2,1)}, u32[]{:S(2)}) copy-start(bf16[2,8192,32]{1,2,0:T(8,128)(2,1)} %param.36) | copy-start | bytes 3145732
  320.9 11.0 %copy-start.2 = (bf16[1024,8192]{1,0:T(8,128)(2,1)S(1)}, bf16[1024,8192]{1,0:T(8,128)(2,1)}, u32[]{:S(2)}) copy-start(bf16[1024,8192]{1,0:T(8,128)(2,1)} %all-gather.5.cloned.1.call-done) | copy-start | bytes 50331652
  336.9 8.2 %copy-start.11 = (f32[256]{0:T(256)S(1)}, f32[256]{0:T(256)}, u32[]{:S(2)}) copy-start(f32[256]{0:T(256)} %param.35) | copy-start | bytes 3076
  338.5 36.6 %all-to-all-start.2 = ((bf16[16,2,32,1024]{3,2,1,0:T(8,128)(2,1)}), bf16[16,2,32,1024]{3,2,1,0:T(8,128)(2,1)S(1)}, u32[]{:S(2)}, u32[]{:S(2)}) async-start(bf16[16,2,32,1024]{3,2,1,0:T(8,128)(2,1)} %broadcast_in_dim.33), calls=%async_computation.3 | async-start | bytes 4194304 | tf_op jit(solution)/shard_map/all_to_all | solution.py:23
  388.5 7.4 %copy-start.1 = (bf16[5120,320]{0,1:T(8,128)(2,1)S(1)}, bf16[5120,320]{0,1:T(8,128)(2,1)}, u32[]{:S(2)}) copy-start(bf16[5120,320]{0,1:T(8,128)(2,1)} %param.29) | copy-start | bytes 9830404
Sparse Core Ops, SparseCore 0:
  24.8 58.5 all-gather.2
  100.2 85.7 reduce-scatter.1
  212.4 108.4 all-gather.4
where the time goes:
time: 403 us; the launch traced here: 402 us
  waiting for transfers between devices  281 us (70%)
  matrix products  69.6 us (17%)
  local copies, waits for them, and re-layouts  17 us (4%)
  starting transfers between devices  14.4 us (4%)
  between operations  13.3 us (3%)
  other arithmetic  7.39 us (2%)
    all_gather x1, waiting for transfers between devices, shards(): shard_rows = lax.all_gather(llm_normed, 'mp', axis=0, tiled=True)  109 us
    reduce_scatter x1, waiting for transfers between devices, shards(): lax.psum_scatter(jnp.dot(hidden, merge_w2, preferred_element_type=jnp.flo...  79.8 us
    all_gather x1, waiting for transfers between devices, shards(): rows_all = lax.all_gather(merged, 'mp', axis=0, tiled=True)  58.6 us
    all_to_all x1, waiting for transfers between devices, copy_for_each(): lax.all_to_all(jnp.broadcast_to(x[None], (size, *x.shape)), axis, 0, 0, t...  20 us
    dot_general x1, matrix products, shards(): jnp.dot(hidden, merge_w2, preferred_element_type=jnp.float32)  16.7 us
    all_to_all x1, waiting for transfers between devices, shards(): lax.all_to_all(buffer, 'dp', split_axis=0, concat_axis=0, tiled=True)  13.6 us
    dot_general x1, matrix products, shards(): jnp.dot(shard_rows, kv_w[1], preferred_element_type=jnp.float32)  10.9 us
    dot_general x1, matrix products, shards(): jnp.dot(shard_rows, q_w, preferred_element_type=jnp.float32)  10 us
  transfers between devices with their start and end apart: 6, of which 5 were waited for; matrix products, arithmetic and copies ran while one was open for 4% of the time, Pallas kernels for 0%

commit v1 on v0

--- a/solution.py
+++ b/solution.py
@@ -1,6 +1,8 @@
 import jax
 import jax.numpy as jnp
 from jax import lax
+from jax.experimental import pallas as pl
+from jax.experimental.pallas import tpu as pltpu
 from jax.sharding import PartitionSpec as P
 
 VHD = 80
@@ -59,7 +61,288 @@
         + jnp.dot(mixture, vit_out_w, preferred_element_type=jnp.float32)
     ).astype(jnp.bfloat16)
     merged = rms_norm(residual, merge_norm).astype(jnp.bfloat16)
-    return merged.reshape(blocks * width // 4, 4 * patches.shape[1])
+    return merged
+
+
+MESH = pl.DeviceIdType.MESH
+NT = (((1,), (1,)), ((), ()))
+
+
+class Copies:
+    def __init__(self, send, recv, local):
+        self.send, self.recv, self.local = send, recv, local
+        self.n, self.m = 0, 0
+        self.sent = []
+
+    def remote(self, src, dst, dev):
+        k = self.n
+        self.n += 1
+        c = pltpu.make_async_remote_copy(
+            src_ref=src, dst_ref=dst, send_sem=self.send.at[k], recv_sem=self.recv.at[k],
+            device_id=dev, device_id_type=MESH)
+        c.start()
+        self.sent.append(c)
+        return c
+
+    def here(self, src, dst):
+        k = self.m
+        self.m += 1
+        c = pltpu.make_async_copy(src, dst, self.local.at[k])
+        c.start()
+        return c
+
+    def drain(self):
+        for c in self.sent:
+            c.wait_send()
+        self.sent = []
+
+
+def places():
+    mp, dp = lax.axis_index("mp"), lax.axis_index("dp")
+    y, x = mp // 4, lax.rem(mp, 4)
+    X = lambda s: (dp, y * 4 + lax.rem(x + s + 4, 4))
+    Y = lambda s: (dp, lax.rem(y + s + 4, 4) * 4 + x)
+    Z = lambda s: (lax.rem(dp + 2 * s + 8, 8), mp)
+    other = (dp + 1 - 2 * lax.rem(dp, 2), mp)
+    return dp, y, x, X, Y, Z, other
+
+
+def meet(devs):
+    barrier = pltpu.get_barrier_semaphore()
+    for d in devs:
+        pl.semaphore_signal(barrier, inc=1, device_id=d, device_id_type=MESH)
+    pl.semaphore_wait(barrier, len(devs))
+
+
+N1 = 104
+
+
+def merger_kernel(m, w1, b1, w2, b2, qw, kvt, kvb, info,
+                  e_out, wq, wkv, kb, info_out,
+                  G, w1v, H, W2, KVX, PO, PR, PL, PW, RO, RN, send, recv, local):
+    dp, y, x, X, Y, Z, other = places()
+    md = lambda v, s: lax.rem(v + s + 4, 4)
+    e = dp
+    z = dp // 2
+    cp = Copies(send, recv, local)
+    meet([X(1), X(2), X(3), Y(1), Y(2), Y(3), Z(1), Z(-1), other])
+    A, B = pl.ds(0, 2), pl.ds(2, 2)
+    a1 = {s: cp.remote(m.at[A], G.at[A, y, x], X(s)) for s in (1, -1)}
+    c1 = {s: cp.remote(m.at[B], G.at[B, y, x], Y(s)) for s in (1, -1)}
+    a2 = {(0, s): cp.remote(m.at[A], G.at[A, y, x], Y(s)) for s in (1, -1)}
+    c2 = {(0, s): cp.remote(m.at[B], G.at[B, y, x], X(s)) for s in (1, -1)}
+    loc = [cp.here(m, G.at[:, y, x]), cp.here(w1, w1v)]
+    cols = lambda xd: pl.ds(pl.multiple_of(2048 * xd + 256 * e, 256), 256)
+    mine = pl.ds(pl.multiple_of(256 * e, 256), 256)
+    wx = []
+    for s in (1, 3, 2):
+        xd = md(x, s)
+        wx.append(cp.remote(w2.at[:, cols(xd)], W2.at[x, :, mine], X(s)))
+    for s in (1, 3, 2):
+        xd = md(x, s)
+        wx.append(cp.remote(qw.at[cols(xd), :], wq.at[x, mine, :], X(s)))
+        wx.append(cp.remote(kvt.at[:, :, cols(xd)], KVX.at[x], X(s)))
+        wx.append(cp.remote(kvb, kb.at[y, x], X(s)))
+        wx.append(cp.remote(info, info_out.at[x], X(s)))
+    wl = [cp.here(w2.at[:, cols(x)], W2.at[x, :, mine]),
+          cp.here(qw.at[cols(x), :], wq.at[x, mine, :]),
+          cp.here(kvt.at[:, :, cols(x)], KVX.at[x]),
+          cp.here(kvb, kb.at[y, x]),
+          cp.here(info, info_out.at[x])]
+
+    af, cf = {}, {}
+    for s in (1, -1):
+        a1[s].wait_recv()
+        xs, j = md(x, -s), 0 if s == 1 else 1
+        af[s] = cp.remote(G.at[j, y, xs], G.at[j, y, xs], X(s))
+        for t in (1, -1):
+            a2[(-s, t)] = cp.remote(G.at[A, y, xs], G.at[A, y, xs], Y(t))
+        c1[s].wait_recv()
+        ys, j = md(y, -s), 2 if s == 1 else 3
+        cf[s] = cp.remote(G.at[j, ys, x], G.at[j, ys, x], Y(s))
+        for t in (1, -1):
+            c2[(-s, t)] = cp.remote(G.at[B, ys, x], G.at[B, ys, x], X(t))
+    last = []
+
+    def pass_on(p):
+        for t in (1, -1):
+            a2[(p, t)].wait_recv()
+            xs, ys, j = md(x, p), md(y, -t), 0 if t == 1 else 1
+            last.append(cp.remote(G.at[j, ys, xs], G.at[j, ys, xs], Y(t)))
+            c2[(p, t)].wait_recv()
+            ys, xs, j = md(y, p), md(x, -t), 2 if t == 1 else 3
+            last.append(cp.remote(G.at[j, ys, xs], G.at[j, ys, xs], X(t)))
+
+    pass_on(0)
+    for c in wx[:3]:
+        c.wait_recv()
+    wl[0].wait()
+    first, second = pl.ds(0, 2), pl.ds(2, 2)
+    bands = lambda r: pl.ds(pl.multiple_of(256 * r, 256), 256)
+
+    def piece(name, r, half=None):
+        if name == "w2":
+            h = pl.ds(0, 4) if half is None else (first, second)[half]
+            return W2.at[h, :, bands(r)]
+        if name == "q":
+            h = pl.ds(0, 4) if half is None else (first, second)[half]
+            return wq.at[h, bands(r), :]
+        h = pl.ds(0, 4) if half is None else (first, second)[half]
+        return wkv.at[h, :, :, bands(r)]
+
+    zs, ds_, zf, at = {}, {}, {}, {}
+
+    def z_start(name):
+        zs[name] = {s: cp.remote(piece(name, e), piece(name, e), Z(s)) for s in (1, -1)}
+        ds_[name] = [cp.remote(piece(name, e), piece(name, e), other)]
+
+    def z_mid(name):
+        zf[name] = {}
+        for s in (1, -1):
+            zs[name][s].wait_recv()
+            r, h = lax.rem(e - 2 * s + 8, 8), 0 if s == 1 else 1
+            zf[name][s] = cp.remote(piece(name, r, h), piece(name, r, h), Z(s))
+            ds_[name].append(cp.remote(piece(name, r), piece(name, r), other))
+
+    def z_end(name):
+        for s in (1, -1):
+            zf[name][s].wait_recv()
+        r = lax.rem(e + 4, 8)
+        ds_[name].append(cp.remote(piece(name, r), piece(name, r), other))
+
+    def z_all(name):
+        for c in ds_[name]:
+            c.wait_recv()
+
+    z_start("w2")
+    for c in wx[3:]:
+        c.wait_recv()
+    for c in wl[1:]:
+        c.wait()
+    z_start("q")
+    ky = []
+    for s in (1, 2, 3):
+        yd = md(y, s)
+        ky.append(cp.remote(KVX.at[:, yd], wkv.at[y, :, :, mine], Y(s)))
+        ky.append(cp.remote(kb.at[y], kb.at[y], Y(s)))
+    kl = cp.here(KVX.at[:, y], wkv.at[y, :, :, mine])
+    for s in (1, -1):
+        af[s].wait_recv()
+        cf[s].wait_recv()
+    xf, yf = md(x, 2), md(y, 2)
+    for t in (1, -1):
+        a2[(2, t)] = cp.remote(G.at[A, y, xf], G.at[A, y, xf], Y(t))
+        c2[(2, t)] = cp.remote(G.at[B, yf, x], G.at[B, yf, x], X(t))
+    pass_on(-1)
+    pass_on(1)
+    z_mid("w2")
+    for c in ky:
+        c.wait_recv()
+    kl.wait()
+    z_start("kv")
+    pass_on(2)
+    for c in last:
+        c.wait_recv()
+    for c in loc:
+        c.wait()
+    for g in range(4):
+        acc = None
+        for j in range(4):
+            p = lax.dot_general(w1v[:, 1280 * j:1280 * (j + 1)], G[j, g].reshape(128, 1280), NT,
+                                preferred_element_type=jnp.float32)
+            acc = p if acc is None else acc + p
+        v = acc + b1[...]
+        v = 0.5 * v * (1.0 + lax.erf(v * (0.5 ** 0.5)))
+        H[x, :, 128 * g:128 * (g + 1)] = v.astype(jnp.bfloat16)
+    h1 = {s: cp.remote(H.at[x], H.at[x], X(s)) for s in (1, -1)}
+    z_end("w2")
+    z_mid("q")
+    z_mid("kv")
+    h2 = []
+    for s in (1, -1):
+        h1[s].wait_recv()
+        xs, r = md(x, -s), pl.ds(0, 160) if s == 1 else pl.ds(160, 160)
+        h2.append(cp.remote(H.at[xs, r, :], H.at[xs, r, :], X(s)))
+    z_all("w2")
+    for c in h2:
+        c.wait_recv()
+
+    def product(g, put):
+        hg = H[:, :, pl.ds(pl.multiple_of(128 * g, 128), 128)].reshape(1280, 128).T
+        for n in range(4):
+            cs = slice(512 * n, 512 * (n + 1))
+            put(cs, jnp.dot(hg, W2[:, :, cs].reshape(1280, 512), preferred_element_type=jnp.float32))
+
+    def to(ref):
+        def put(cs, v):
+            ref[:, cs] = v.astype(ref.dtype)
+        return put
+
+    product(md(y, 2), to(PO))
+    lo, hi = pl.ds(0, 64), pl.ds(64, 64)
+    o = {1: cp.remote(PO.at[lo], RO.at[0], Y(1)), -1: cp.remote(PO.at[hi], RO.at[1], Y(-1))}
+    product(md(y, 1), to(PR))
+    n1 = [cp.remote(PR.at[hi], RN.at[0, hi], Y(1))]
+    product(md(y, -1), to(PL))
+    n1.append(cp.remote(PL.at[lo], RN.at[1, lo], Y(-1)))
+    o[1].wait_recv()
+    PR[0:64, :] = (PR[0:64, :].astype(jnp.float32) + RO[0].astype(jnp.float32)).astype(jnp.bfloat16)
+    n1.append(cp.remote(PR.at[lo], RN.at[0, lo], Y(1)))
+    o[-1].wait_recv()
+    PL[64:128, :] = (PL[64:128, :].astype(jnp.float32) + RO[1].astype(jnp.float32)).astype(jnp.bfloat16)
+    n1.append(cp.remote(PL.at[hi], RN.at[1, hi], Y(-1)))
+    product(y, to(PW))
+    z_end("q")
+    z_end("kv")
+    for c in n1:
+        c.wait_recv()
+    total = PW[...] + RN[0].astype(jnp.float32) + RN[1].astype(jnp.float32)
+    e_out[...] = (total + b2[:, pl.ds(pl.multiple_of(2048 * x, 2048), 2048)]).astype(jnp.bfloat16)
+    z_all("q")
+    z_all("kv")
+    cp.drain()
+
+
+def merger(m, w1, b1, w2, b2, qw, kvt, kvb, info):
+    bf, f32 = jnp.bfloat16, jnp.float32
+    V, ANY = pl.BlockSpec(memory_space=pltpu.VMEM), pl.BlockSpec(memory_space=pl.ANY)
+    S = jax.ShapeDtypeStruct
+    return pl.pallas_call(
+        merger_kernel,
+        out_shape=(S((128, 2048), bf), S((4, 2048, 256), bf), S((4, 4, 16, 2048), bf), S((4, 4, 8, 128), f32),
+                   S((4, 8, 128), jnp.int32)),
+        in_specs=[V, ANY, V, ANY, V, ANY, ANY, V, V],
+        out_specs=[V] * 5,
+        scratch_shapes=[
+            pltpu.VMEM((4, 4, 4, 32, 1280), bf),
+            pltpu.VMEM((320, 5120), bf),
+            pltpu.VMEM((4, 320, 512), bf),
+            pltpu.VMEM((4, 320, 2048), bf),
+            pltpu.VMEM((4, 4, 16, 256), bf),
+            pltpu.VMEM((128, 2048), bf),
+            pltpu.VMEM((128, 2048), bf),
+            pltpu.VMEM((128, 2048), bf),
+            pltpu.VMEM((128, 2048), f32),
+            pltpu.VMEM((2, 64, 2048), bf),
+            pltpu.VMEM((2, 128, 2048), bf),
+            pltpu.SemaphoreType.DMA((N1,)),
+            pltpu.SemaphoreType.DMA((N1,)),
+            pltpu.SemaphoreType.DMA((16,)),
+        ],
+        compiler_params=pltpu.CompilerParams(collective_id=1, has_side_effects=True, vmem_limit_bytes=60000000),
+        name="merger",
+    )(m, w1, b1, w2, b2, qw, kvt, kvb, info)
+
+
+def prepared(merged, owner, slot_of_row, kv_w, kv_b):
+    x = lax.rem(lax.axis_index("mp"), 4)
+    m = merged.reshape(32, 4, 1280).transpose(1, 0, 2)
+    kvt = kv_w.transpose(0, 2, 1).reshape(2, 8, 4, 8192).transpose(2, 0, 1, 3).reshape(4, 16, 8192)
+    kvb = jnp.pad(kv_b.reshape(2, 8, 4).transpose(2, 0, 1).reshape(4, 16), ((0, 4), (0, 112)))
+    zero = jnp.zeros((8, 128), jnp.int32)
+    info = lax.dynamic_update_slice(zero, owner.reshape(1, 32), (0, 32 * x))
+    info = lax.dynamic_update_slice(info, slot_of_row, (1 + x // 2, 64 * lax.rem(x, 2)))
+    return m, kvt, kvb, info
 
 
 def shards(
@@ -83,22 +366,19 @@
     kv_w,
     kv_b,
 ):
-    merged = vision_block(
+    merged_rows = vision_block(
         patches, window_ids, vit_norm, vit_qkv_w, vit_qkv_b, vit_out_w, merge_norm
     )
     own_index = lax.axis_index("mp")
-    rows_all = lax.all_gather(merged, "mp", axis=0, tiled=True)
-    hidden = jax.nn.gelu(
-        jnp.dot(rows_all, merge_w1, preferred_element_type=jnp.float32) + merge_b1,
-        approximate=False,
-    ).astype(jnp.bfloat16)
-    own_rows = lax.psum_scatter(
-        jnp.dot(hidden, merge_w2, preferred_element_type=jnp.float32).astype(jnp.bfloat16),
-        "mp",
-        scatter_dimension=0,
-        tiled=True,
-    ).astype(jnp.float32)
-    embedded = (own_rows + merge_b2).astype(jnp.bfloat16)
+    merged = merged_rows
+    m, kvt, kvb, info = prepared(merged, owner, slot_of_row, kv_w, kv_b)
+    part, wq, wkv, kb, info_all = merger(
+        m, merge_w1.T, merge_b1[:, None], merge_w2, merge_b2[None], q_w, kvt, kvb, info
+    )
+    embedded = lax.all_to_all(
+        part.reshape(4, 32, 2048), "mp", 0, 0, tiled=True,
+        axis_index_groups=[[4 * i + j for j in range(4)] for i in range(4)],
+    ).transpose(1, 0, 2).reshape(32, 8192)
     seq_rows = text_embeds.shape[0]
     groups = lax.axis_size("dp")
     capacity = seq_rows // groups

time: 403 us -> 345 us (0.86)
  waiting for transfers between devices: 281 us -> 151 us
  Pallas kernels: 0 us -> 89.3 us
  matrix products: 69.6 us -> 47 us
    pallas_call x0 -> x1, Pallas kernels: none -> 89.3 us  [merger(): pl.pallas_call(merger_kernel, out_shape=(S((128, 2048), bf), S((4, 2048,...]
    reduce_scatter x1 -> x0, waiting for transfers between devices: 79.8 us -> none  [shards(): lax.psum_scatter(jnp.dot(hidden, merge_w2, preferred_element_type=jnp.flo...]
    all_gather x1 -> x0, waiting for transfers between devices: 58.6 us -> none  [shards(): rows_all = lax.all_gather(merged, 'mp', axis=0, tiled=True)]
    dot_general x1 -> x0, matrix products: 16.7 us -> none  [shards(): jnp.dot(hidden, merge_w2, preferred_element_type=jnp.float32)]
    all_to_all x0 -> x1, waiting for transfers between devices: none -> 6.99 us  [shards(): lax.all_to_all(part.reshape(4, 32, 2048), 'mp', 0, 0, tiled=True, axis_in...]
  transfers between devices with their start and end apart: 6 -> 5, of which waited for: 5 -> 5; matrix products, arithmetic and copies ran while one was open for 4% -> 4% of each run, Pallas kernels for 0% -> 0%
where the time goes in v1:
time: 345 us; the launch traced here: 344 us
  waiting for transfers between devices  151 us (44%)
  Pallas kernels  89.3 us (26%)
  matrix products  47 us (14%)
  local copies, waits for them, and re-layouts  17.7 us (5%)
  starting transfers between devices  16.3 us (5%)
  between operations  13.7 us (4%)
  other arithmetic  9.03 us (3%)
    all_gather x1, waiting for transfers between devices, shards(): shard_rows = lax.all_gather(llm_normed, 'mp', axis=0, tiled=True)  107 us
    pallas_call x1, Pallas kernels, merger(): pl.pallas_call(merger_kernel, out_shape=(S((128, 2048), bf), S((4, 2048,...  89.3 us
    all_to_all x1, waiting for transfers between devices, copy_for_each(): lax.all_to_all(jnp.broadcast_to(x[None], (size, *x.shape)), axis, 0, 0, t...  20 us
    all_to_all x1, waiting for transfers between devices, shards(): lax.all_to_all(buffer, 'dp', split_axis=0, concat_axis=0, tiled=True)  13.5 us
    dot_general x1, matrix products, shards(): jnp.dot(shard_rows, kv_w[1], preferred_element_type=jnp.float32)  10.9 us
    dot_general x1, matrix products, shards(): jnp.dot(shard_rows, q_w, preferred_element_type=jnp.float32)  10 us
    all_to_all x1, waiting for transfers between devices, shards(): lax.all_to_all(part.reshape(4, 32, 2048), 'mp', 0, 0, tiled=True, axis_in...  6.99 us
  transfers between devices with their start and end apart: 5, of which 5 were waited for; matrix products, arithmetic and copies ran while one was open for 4% of the time, Pallas kernels for 0%

profile of v1, /device:TPU:0, one launch (start us, length us, event | category | flops | bytes accessed | tf_op | source)
XLA Modules:
  0.0 344.3 jit_solution(13372689561262032332)
XLA Ops:
  6.5 0.9 broadcast_compare_fusion
  7.4 1.1 fusion.25
  8.6 3.5 %fusion.10 = bf16[128,1920]{1,0:T(8,128)(2,1)S(1)} fusion(bf16[1280,1920]{1,0:T(8,128)(2,1)} %param.25, f32[1920]{0:T(1024)} %param.26, bf16[128,1280]{1,0:T(8,128)(2,1)} %param.19, f32[1280]{0:T(1024)} %param.24, f32[128]{0:T(128)S(1)} %add_rsqrt_fusion.2), kind=kOutput, calls=%fused_computation.21 | convolution fusion | flops 630292480 | bytes 5747712 | tf_op jit(solution)/shard_map/dot_general | solution.py:39
  12.8 1.1 fusion.18
  13.8 2.1 convolution_convert_fusion.1
  16.0 1.5 multiply_reduce_fusion
  19.7 1.6 copy.87
  22.9 89.3 %merger.1 = (bf16[128,2048]{1,0:T(8,128)(2,1)}, bf16[4,2048,256]{2,1,0:T(8,128)(2,1)}, bf16[4,4,16,2048]{3,2,1,0:T(8,128)(2,1)}, f32[4,4,8,128]{3,2,1,0:T(8,128)}, s32[4,8,128]{2,1,0:T(8,128)}) custom-call(bf16[4,32,1280]{2,1,0:T(8,128)(2,1)} %bitcast.132, bf16[320,5120]{1,0:T(8,128)(2,1)} %bitcast.126, f32[320,1]{1,0:T(8,128)} %broadcast_in_dim.45.b1, ...), custom_call_target="tpu_custom_call" | custom-call | tf_op jit(solution)/shard_map/merger/pallas_call | solution.py:310
  112.3 3.9 %all-to-all-start.1 = ((bf16[4,32,2048]{2,1,0:T(8,128)(2,1)}), bf16[4,32,2048]{2,1,0:T(8,128)(2,1)S(1)}, u32[]{:S(2)}, u32[]{:S(2)}) async-start(bf16[4,32,2048]{2,1,0:T(8,128)(2,1)} %bitcast.133), calls=%async_computation.1 | async-start | bytes 1048576 | tf_op jit(solution)/shard_map/all_to_all | solution.py:378
  117.2 7.0 %all-to-all-done.1 = bf16[4,32,2048]{2,1,0:T(8,128)(2,1)S(1)} async-done(((bf16[4,32,2048]{2,1,0:T(8,128)(2,1)}), bf16[4,32,2048]{2,1,0:T(8,128)(2,1)S(1)}, u32[]{:S(2)}, u32[]{:S(2)}) %all-to-all-start.1) | async-done | bytes 524320 | tf_op jit(solution)/shard_map/all_to_all | solution.py:378
  124.2 3.3 all-to-all-start
  127.6 1.5 fusion.2
  129.1 3.5 %all-to-all-done = s32[8,1,8]{2,1,0:T(1,128)S(1)} async-done(((s32[8,1,8]{2,1,0:T(1,128)}), s32[8,1,8]{2,1,0:T(1,128)S(1)}, u32[]{:S(2)}, u32[]{:S(2)}) %all-to-all-start) | async-done | bytes 288 | tf_op jit(solution)/shard_map/all_to_all | solution.py:399
  132.7 3.6 %all-to-all-start.2 = ((bf16[8,8,8192]{2,1,0:T(8,128)(2,1)}), bf16[8,8,8192]{2,1,0:T(8,128)(2,1)S(1)}, u32[]{:S(2)}, u32[]{:S(2)}) async-start(bf16[8,8,8192]{2,1,0:T(8,128)(2,1)} %fusion.2), calls=%async_computation.2 | async-start | bytes 2097152 | tf_op jit(solution)/shard_map/all_to_all | solution.py:398
  138.6 13.5 %all-to-all-done.2 = bf16[8,8,8192]{2,1,0:T(8,128)(2,1)S(1)} async-done(((bf16[8,8,8192]{2,1,0:T(8,128)(2,1)}), bf16[8,8,8192]{2,1,0:T(8,128)(2,1)S(1)}, u32[]{:S(2)}, u32[]{:S(2)}) %all-to-all-start.2) | async-done | bytes 1048608 | tf_op jit(solution)/shard_map/all_to_all | solution.py:398
  152.1 1.2 gather_fusion.1
  153.3 1.8 fusion.11
  155.2 2.7 fusion.13
  157.9 107.1 %all-gather.2.cloned.1.call-done = bf16[1024,8192]{1,0:T(8,128)(2,1)} async-done(((bf16[64,8192]{1,0:T(8,128)(2,1)}), bf16[1024,8192]{1,0:T(8,128)(2,1)}) %all-gather.2.cloned.1.call-update) | async-done | bytes 16777232 | tf_op jit(solution)/shard_map/all_gather | solution.py:408
  265.0 10.9 %fusion.21 = bf16[1,32,1024]{2,1,0:T(8,128)(2,1)S(1)} fusion(bf16[1024,8192]{1,0:T(8,128)(2,1)} %all-gather.2.cloned.1.call-done, bf16[2,8192,32]{1,2,0:T(8,128)(2,1)S(1)} %copy-done.4, f32[32]{0:T(128)S(1)} %get-tuple-element.10), kind=kOutput, calls=%fused_computation.37 | convolution fusion | flops 536936448 | bytes 17367552 | tf_op jit(solution)/shard_map/dot_general | solution.py:413
  276.0 5.0 %fusion.22 = bf16[1,32,1024]{2,1,0:T(8,128)(2,1)S(1)} fusion(bf16[1024,8192]{1,0:T(8,128)(2,1)S(1)} %copy-done.2, bf16[2,8192,32]{1,2,0:T(8,128)(2,1)S(1)} %copy-done.4, f32[32]{0:T(128)S(1)} %get-tuple-element.9), kind=kOutput, calls=%fused_computation.38 | convolution fusion | flops 536936448 | bytes 17367552 | tf_op jit(solution)/shard_map/dot_general | solution.py:412
  281.1 1.6 broadcast_in_dim.42
  282.6 5.3 %all-to-all-start.3 = ((bf16[16,2,32,1024]{3,2,1,0:T(8,128)(2,1)}), bf16[16,2,32,1024]{3,2,1,0:T(8,128)(2,1)}, u32[]{:S(2)}, u32[]{:S(2)}) async-start(bf16[16,2,32,1024]{3,2,1,0:T(8,128)(2,1)} %broadcast_in_dim.42), calls=%async_computation.3 | async-start | bytes 4194304 | tf_op jit(solution)/shard_map/all_to_all | solution.py:25
  288.0 1.3 iota_compare_fusion
  289.3 10.0 %fusion.14 = bf16[1024,256]{0,1:T(8,128)(2,1)} fusion(bf16[1024,8192]{1,0:T(8,128)(2,1)} %all-gather.2.cloned.1.call-done, bf16[8192,256]{1,0:T(8,128)(2,1)} %qw.1, f32[256]{0:T(256)S(1)} %copy-done.13), kind=kOutput, calls=%fused_computation.26 | convolution fusion | flops 4295491584 | bytes 21496832 | tf_op jit(solution)/shard_map/dot_general | solution.py:411
  299.3 20.0 %all-to-all-done.3 = bf16[16,2,32,1024]{3,2,1,0:T(8,128)(2,1)} async-done(((bf16[16,2,32,1024]{3,2,1,0:T(8,128)(2,1)}), bf16[16,2,32,1024]{3,2,1,0:T(8,128)(2,1)}, u32[]{:S(2)}, u32[]{:S(2)}) %all-to-all-start.3) | async-done | bytes 2097184 | tf_op jit(solution)/shard_map/all_to_all | solution.py:25
  319.3 1.8 fusion.52
  321.2 1.2 squeeze.37
  322.8 2.3 constant_dynamic-slice_fusion
  325.6 6.6 %fusion.54 = (f32[2,1024]{1,0:T(2,128)S(1)}, f32[2,1024,1024]{1,2,0:T(8,128)}) fusion(pred[1024,1024]{0,1:T(8,128)(4,1)} %iota_compare_fusion, bf16[1024,2,128]{0,2,1:T(8,128)(2,1)S(1)} %bitcast.142, bf16[128,1,1024]{0,2,1:T(8,128)(2,1)S(1)} %copy.71), kind=kOutput, calls=%fused_computation.92 | convolution fusion | flops 545260544 | bytes 10231808 | tf_op jit(solution)/shard_map/sub | solution.py:436
  332.2 4.3 %fusion.15 = bf16[128,2,1024]{2,0,1:T(8,128)(2,1)S(1)} fusion(f32[2,1024,1024]{1,2,0:T(8,128)} %get-tuple-element.14, f32[2,1024]{1,0:T(2,128)S(1)} %get-tuple-element.13, bf16[128,1,1024]{2,1,0:T(2,128)(2,1)S(1)} %get-tuple-element.16), kind=kOutput, calls=%fused_computation.27 | convolution fusion | flops 541327360 | bytes 9183232 | tf_op jit(solution)/shard_map/hqk,dk->qhd/dot_general | solution.py:438
  336.4 1.0 copy.74
  (66 shorter events, 8.9 us)
Async XLA Ops:
  6.5 9.5 %copy-start = (bf16[640,1280]{1,0:T(8,128)(2,1)S(1)}, bf16[640,1280]{1,0:T(8,128)(2,1)}, u32[]{:S(2)}) copy-start(bf16[640,1280]{1,0:T(8,128)(2,1)} %param.27) | copy-start | bytes 4915204
  8.6 7.5 %copy-start.5 = (bf16[128,1280]{1,0:T(8,128)(2,1)S(1)}, bf16[128,1280]{1,0:T(8,128)(2,1)}, u32[]{:S(2)}) copy-start(bf16[128,1280]{1,0:T(8,128)(2,1)} %param.19) | copy-start | bytes 983044
  12.1 5.4 %copy-start.8 = (f32[1280]{0:T(1024)S(1)}, f32[1280]{0:T(1024)}, u32[]{:S(2)}) copy-start(f32[1280]{0:T(1024)} %param.28) | copy-start | bytes 15364
  12.4 6.1 %copy-start.11 = (f32[320]{0:T(512)S(1)}, f32[320]{0:T(512)}, u32[]{:S(2)}) copy-start(f32[320]{0:T(512)} %param.30) | copy-start | bytes 3844
  12.4 6.9 %copy-start.3 = (bf16[2,8192,32]{1,2,0:T(8,128)(2,1)S(1)}, bf16[2,8192,32]{1,2,0:T(8,128)(2,1)}, u32[]{:S(2)}) copy-start(bf16[2,8192,32]{1,2,0:T(8,128)(2,1)} %param.36) | copy-start | bytes 3145732
  16.0 5.2 %copy-start.10 = (f32[2,32]{1,0:T(2,128)S(1)}, f32[2,32]{1,0:T(2,128)}, u32[]{:S(2)}) copy-start(f32[2,32]{1,0:T(2,128)} %param.37) | copy-start | bytes 772
  16.0 6.0 %copy-start.9 = (s32[32,1]{0,1:T(1,128)S(1)}, s32[32,1]{0,1:T(1,128)}, u32[]{:S(2)}) copy-start(s32[32,1]{0,1:T(1,128)} %param.21) | copy-start | bytes 388
  16.0 6.1 %copy-start.12 = (s32[1,64]{1,0:T(1,128)S(1)}, s32[1,64]{1,0:T(1,128)}, u32[]{:S(2)}) copy-start(s32[1,64]{1,0:T(1,128)} %param.22) | copy-start | bytes 772
  22.3 0.6 copy-start.7
  112.3 12.0 %all-to-all-start.1 = ((bf16[4,32,2048]{2,1,0:T(8,128)(2,1)}), bf16[4,32,2048]{2,1,0:T(8,128)(2,1)S(1)}, u32[]{:S(2)}, u32[]{:S(2)}) async-start(bf16[4,32,2048]{2,1,0:T(8,128)(2,1)} %bitcast.133), calls=%async_computation.1 | async-start | bytes 1048576 | tf_op jit(solution)/shard_map/all_to_all | solution.py:378
  124.2 8.5 %all-to-all-start = ((s32[8,1,8]{2,1,0:T(1,128)}), s32[8,1,8]{2,1,0:T(1,128)S(1)}, u32[]{:S(2)}, u32[]{:S(2)}) async-start(s32[8,1,8]{2,1,0:T(1,128)} %bitcast.1), calls=%async_computation | async-start | bytes 8192 | tf_op jit(solution)/shard_map/all_to_all | solution.py:399
  132.7 19.4 %all-to-all-start.2 = ((bf16[8,8,8192]{2,1,0:T(8,128)(2,1)}), bf16[8,8,8192]{2,1,0:T(8,128)(2,1)S(1)}, u32[]{:S(2)}, u32[]{:S(2)}) async-start(bf16[8,8,8192]{2,1,0:T(8,128)(2,1)} %fusion.2), calls=%async_computation.2 | async-start | bytes 2097152 | tf_op jit(solution)/shard_map/all_to_all | solution.py:398
  136.2 128.8 %all-gather.2.cloned.1.call-start = ((), (), s32[]{:S(2)}) async-start(), calls=%async_computation.4 | async-start | bytes 17825792 | tf_op jit(solution)/shard_map/all_gather | solution.py:408
  152.1 3.1 copy-start.6
  153.3 111.7 %copy-start.4 = (bf16[2,8192,32]{1,2,0:T(8,128)(2,1)S(1)}, bf16[2,8192,32]{1,2,0:T(8,128)(2,1)}, u32[]{:S(2)}) copy-start(bf16[2,8192,32]{1,2,0:T(8,128)(2,1)} %param.36) | copy-start | bytes 3145732
  265.0 11.0 %copy-start.2 = (bf16[1024,8192]{1,0:T(8,128)(2,1)S(1)}, bf16[1024,8192]{1,0:T(8,128)(2,1)}, u32[]{:S(2)}) copy-start(bf16[1024,8192]{1,0:T(8,128)(2,1)} %all-gather.2.cloned.1.call-done) | copy-start | bytes 50331652
  281.0 8.2 %copy-start.13 = (f32[256]{0:T(256)S(1)}, f32[256]{0:T(256)}, u32[]{:S(2)}) copy-start(f32[256]{0:T(256)} %param.35) | copy-start | bytes 3076
  282.6 36.7 %all-to-all-start.3 = ((bf16[16,2,32,1024]{3,2,1,0:T(8,128)(2,1)}), bf16[16,2,32,1024]{3,2,1,0:T(8,128)(2,1)}, u32[]{:S(2)}, u32[]{:S(2)}) async-start(bf16[16,2,32,1024]{3,2,1,0:T(8,128)(2,1)} %broadcast_in_dim.42), calls=%async_computation.3 | async-start | bytes 4194304 | tf_op jit(solution)/shard_map/all_to_all | solution.py:25
  319.3 6.3 %copy-start.14 = (bf16[1024,256]{0,1:T(8,128)(2,1)S(1)}, bf16[1024,256]{0,1:T(8,128)(2,1)}, u32[]{:S(2)}) copy-start(bf16[1024,256]{0,1:T(8,128)(2,1)} %fusion.14) | copy-start | bytes 1572868
  332.2 5.3 %copy-start.1 = (bf16[640,1280]{1,0:T(8,128)(2,1)S(1)}, bf16[640,1280]{1,0:T(8,128)(2,1)}, u32[]{:S(2)}) copy-start(bf16[640,1280]{1,0:T(8,128)(2,1)} %param.27) | copy-start | bytes 4915204
Sparse Core Ops, SparseCore 0:
  158.0 106.9 all-gather.1

commit v2 on v1

--- a/solution.py
+++ b/solution.py
@@ -345,6 +345,254 @@
     return m, kvt, kvb, info
 
 
+N2 = 128
+
+
+def language_kernel(part, info, wq, wkv, kb, text, gain, qb,
+                    q_out, kv_out,
+                    T, SB, R, A, SS, SY, SC, Q0, QR, QL, QO, RQO, RQN, KP, RKV, send, recv, local):
+    dp, y, x, X, Y, Z, other = places()
+    md = lambda v, s: lax.rem(v + s + 4, 4)
+    bf, f32 = jnp.bfloat16, jnp.float32
+    mp = y * 4 + x
+    cp = Copies(send, recv, local)
+    group = [(lax.rem(dp + s, 8), mp) for s in range(1, 8)]
+    meet([X(1), X(2), X(3), Y(1), Y(2), Y(3)] + group)
+    quarter = lambda v: pl.ds(pl.multiple_of(2048 * v, 2048), 2048)
+    iota = lambda shape, d: lax.broadcasted_iota(jnp.int32, shape, d)
+
+    tx = [cp.remote(text.at[:, quarter(md(x, s))], T.at[x], X(s)) for s in (1, 3, 2)]
+    tl = cp.here(text.at[:, quarter(x)], T.at[x])
+
+    tab = info[0] + info[1] + info[2] + info[3]
+    own = tab[0:1, :]
+    down = jnp.broadcast_to(own.astype(f32), (128, 128)).T.astype(jnp.int32)
+    r0, r1 = iota((128, 128), 0), iota((128, 128), 1)
+    before = (down == own) & (r0 < r1) & (r0 // 32 == r1 // 32)
+    rank = jnp.sum(before.astype(jnp.int32), axis=0, keepdims=True)
+    target = own * 32 + (iota((1, 128), 1) // 32) * 8 + rank
+    pick = (iota((256, 128), 0) == target).astype(f32).astype(bf)
+    for n in range(4):
+        cs = slice(512 * n, 512 * (n + 1))
+        v = jnp.dot(pick, part[:, cs], preferred_element_type=f32)
+        SB[:, :, cs] = v.astype(bf).reshape(8, 32, 512)
+    v = jnp.dot(pick, jnp.ones((128, 128), bf), preferred_element_type=f32)
+    SB[:, :, 2048:2176] = v.astype(bf).reshape(8, 32, 128)
+    hand = [cp.remote(SB.at[d[0]], R.at[dp], d) for d in group]
+    hl = cp.here(SB.at[dp], R.at[dp])
+
+    choose = []
+    for i in range(2):
+        s = jnp.broadcast_to(tab[1 + i:2 + i, :].astype(f32), (128, 128)).T.astype(jnp.int32)
+        s = jnp.concatenate([s, s], axis=1)
+        lane, row = iota((128, 256), 1), iota((128, 256), 0)
+        hit = ((lane // 32) * 8 + lane % 8 == s) & ((lane % 32) // 8 == row // 64 + 2 * i)
+        choose.append(hit.astype(f32).astype(bf))
+    for c in tx:
+        c.wait_recv()
+    tl.wait()
+    for c in hand:
+        c.wait_recv()
+    hl.wait()
+
+    gx = gain[:, quarter(x)]
+    sq = []
+    yh = {}
+    for i in range(2):
+        seen = jnp.dot(choose[i], R[:, :, 2048:2176].reshape(256, 128), preferred_element_type=f32)
+        filled = seen[:, 0:1] > 0.5
+        total = jnp.zeros((128, 1), f32)
+        for n in range(4):
+            cs = slice(512 * n, 512 * (n + 1))
+            v = jnp.dot(choose[i], R[:, :, cs].reshape(256, 512), preferred_element_type=f32)
+            v = jnp.where(filled, v, T[2 * i:2 * i + 2, :, cs].reshape(128, 512).astype(f32))
+            total = total + jnp.sum(v * v, axis=1, keepdims=True)
+            A[y, 128 * i:128 * (i + 1), cs] = (v * gx[:, cs]).astype(bf)
+        sq.append(total)
+        h = pl.ds(128 * i, 128)
+        if i == 0:
+            yh[(1, 0)] = cp.remote(A.at[y, h], A.at[y, h], Y(1))
+        else:
+            yh[(-1, 1)] = cp.remote(A.at[y, h], A.at[y, h], Y(-1))
+    h = [pl.ds(0, 128), pl.ds(128, 128)]
+    yh[(1, 1)] = cp.remote(A.at[y, h[1]], A.at[y, h[1]], Y(1))
+    yh[(-1, 0)] = cp.remote(A.at[y, h[0]], A.at[y, h[0]], Y(-1))
+    SS[x] = jnp.concatenate([jnp.broadcast_to(t, (128, 128)).T[0:8, :] for t in sq], axis=1)
+    sx = [cp.remote(SS.at[x], SS.at[x], X(s)) for s in (1, 2, 3)]
+
+    def unit(g, i):
+        rows = pl.ds(pl.multiple_of(256 * g + 128 * i, 128), 128)
+        a = A[g, 128 * i:128 * (i + 1), :]
+        prod = lambda s: jnp.dot(a, wq[md(x, s)], preferred_element_type=f32)
+        lo, hi = pl.ds(pl.multiple_of(256 * g + 128 * i, 64), 64), pl.ds(pl.multiple_of(256 * g + 128 * i + 64, 64), 64)
+        QO[rows, :] = prod(2).astype(bf)
+        o = [cp.remote(QO.at[lo], RQO.at[0, lo], X(1)), cp.remote(QO.at[hi], RQO.at[1, hi], X(-1))]
+        KP[rows, :] = lax.dot_general(a, wkv[...].reshape(256, 2048), NT, preferred_element_type=f32).astype(bf)
+        slot = 2 * g + i
+        k = []
+        for s in (2, 1, 3):
+            xd = md(x, s)
+            src = pl.ds(pl.multiple_of(256 * g + 128 * i + 32 * xd, 32), 32)
+            k.append(cp.remote(KP.at[src], RKV.at[x, slot], X(s)))
+        QR[rows, :] = prod(1).astype(bf)
+        n = [cp.remote(QR.at[hi], RQN.at[0, hi], X(1))]
+        QL[rows, :] = prod(-1).astype(bf)
+        n.append(cp.remote(QL.at[lo], RQN.at[1, lo], X(-1)))
+        Q0[rows, :] = prod(0)
+        return g, i, rows, lo, hi, slot, o, k, n
+
+    def relay(u):
+        g, i, rows, lo, hi, slot, o, k, n = u
+        o[0].wait_recv()
+        QR[lo, :] = (QR[lo, :].astype(f32) + RQO[0, lo, :].astype(f32)).astype(bf)
+        n.append(cp.remote(QR.at[lo], RQN.at[0, lo], X(1)))
+        o[1].wait_recv()
+        QL[hi, :] = (QL[hi, :].astype(f32) + RQO[1, hi, :].astype(f32)).astype(bf)
+        n.append(cp.remote(QL.at[hi], RQN.at[1, hi], X(-1)))
+
+    bias = jnp.concatenate([kb[p // 4, p % 4, pl.ds(y, 1), 0:16] for p in range(16)], axis=1)
+
+    def keys(u):
+        g, i, rows, lo, hi, slot, o, k, n = u
+        for c in k:
+            c.wait_recv()
+        m = pl.ds(pl.multiple_of(256 * g + 128 * i + 32 * x, 32), 32)
+        v = KP[m, :].astype(f32)
+        for s in (1, 2, 3):
+            v = v + RKV[md(x, s), slot].astype(f32)
+        sc = SC[m, :]
+        v = v * jnp.concatenate([sc, sc], axis=1) + bias
+        kv_out[m, :] = v.astype(bf)
+        u[7].extend(cp.remote(kv_out.at[m], kv_out.at[m], X(s)) for s in (2, 1, 3))
+
+    def scale(g):
+        v = lax.rsqrt(SY[g] * (1.0 / 8192.0) + 1e-6)
+        for i in range(2):
+            SC[pl.ds(pl.multiple_of(256 * g + 128 * i, 128), 128), :] = jnp.broadcast_to(
+                v[0:1, 128 * i:128 * (i + 1)], (128, 128)).T
+
+    units = [unit(y, 0), unit(y, 1)]
+    for c in sx:
+        c.wait_recv()
+    SY[y] = SS[0] + SS[1] + SS[2] + SS[3]
+    sy = [cp.remote(SY.at[y], SY.at[y], Y(s)) for s in (1, 2, 3)]
+    scale(y)
+    relay(units[0])
+    relay(units[1])
+    keys(units[0])
+    keys(units[1])
+    far = {}
+    up, dn, op = md(y, 1), md(y, -1), md(y, 2)
+    yh[(1, 0)].wait_recv()
+    far[1] = cp.remote(A.at[dn, h[0]], A.at[dn, h[0]], Y(1))
+    yh[(-1, 1)].wait_recv()
+    far[-1] = cp.remote(A.at[up, h[1]], A.at[up, h[1]], Y(-1))
+    units.append(unit(dn, 0))
+    units.append(unit(up, 1))
+    for c in sy:
+        c.wait_recv()
+    for g in (dn, up, op):
+        scale(g)
+    relay(units[2])
+    relay(units[3])
+    keys(units[2])
+    keys(units[3])
+    yh[(1, 1)].wait_recv()
+    units.append(unit(dn, 1))
+    yh[(-1, 0)].wait_recv()
+    units.append(unit(up, 0))
+    relay(units[4])
+    relay(units[5])
+    keys(units[4])
+    keys(units[5])
+    far[1].wait_recv()
+    units.append(unit(op, 0))
+    far[-1].wait_recv()
+    units.append(unit(op, 1))
+    relay(units[6])
+    relay(units[7])
+    keys(units[6])
+    keys(units[7])
+    for u in units:
+        rows, n, k = u[2], u[8], u[7]
+        for c in n:
+            c.wait_recv()
+        sc = SC[rows, :]
+        v = Q0[rows, :] + RQN[0, rows, :].astype(f32) + RQN[1, rows, :].astype(f32)
+        q_out[rows, :] = (v * jnp.concatenate([sc, sc], axis=1) + qb[...]).astype(bf)
+    for u in units:
+        for c in u[7][3:]:
+            c.wait_recv()
+    cp.drain()
+
+
+def language(part, info, wq, wkv, kb, text, gain, qb):
+    bf, f32 = jnp.bfloat16, jnp.float32
+    V, ANY = pl.BlockSpec(memory_space=pltpu.VMEM), pl.BlockSpec(memory_space=pl.ANY)
+    S = jax.ShapeDtypeStruct
+    M = pltpu.VMEM
+    return pl.pallas_call(
+        language_kernel,
+        out_shape=(S((1024, 256), bf), S((1024, 256), bf)),
+        in_specs=[V, V, V, V, V, ANY, V, V],
+        out_specs=[V] * 2,
+        scratch_shapes=[
+            M((4, 64, 2048), bf),
+            M((8, 32, 2176), bf),
+            M((8, 32, 2176), bf),
+            M((4, 256, 2048), bf),
+            M((4, 8, 256), f32),
+            M((4, 8, 256), f32),
+            M((1024, 128), f32),
+            M((1024, 256), f32),
+            M((1024, 256), bf),
+            M((1024, 256), bf),
+            M((1024, 256), bf),
+            M((2, 1024, 256), bf),
+            M((2, 1024, 256), bf),
+            M((1024, 256), bf),
+            M((4, 8, 32, 256), bf),
+            pltpu.SemaphoreType.DMA((N2,)),
+            pltpu.SemaphoreType.DMA((N2,)),
+            pltpu.SemaphoreType.DMA((4,)),
+        ],
+        compiler_params=pltpu.CompilerParams(collective_id=2, has_side_effects=True, vmem_limit_bytes=60000000),
+        name="language",
+    )(part, info, wq, wkv, kb, text, gain, qb)
+
+
+def attention_kernel(q, kv, out):
+    bf, f32 = jnp.bfloat16, jnp.float32
+    c, d = lax.broadcasted_iota(jnp.int32, (256, 128), 0), lax.broadcasted_iota(jnp.int32, (256, 128), 1)
+    spot = (d // 8) * 16 + d % 8
+    keys = jnp.dot(kv[...], (c == spot).astype(f32).astype(bf), preferred_element_type=f32).astype(bf)
+    values = jnp.dot(kv[...], (c == spot + 8).astype(f32).astype(bf), preferred_element_type=f32).astype(bf)
+    for i in range(4):
+        rows = slice(256 * i, 256 * (i + 1))
+        n = 256 * (i + 1)
+        for h in range(2):
+            hs = slice(128 * h, 128 * (h + 1))
+            s = lax.dot_general(q[rows, hs], keys[:n], NT, preferred_element_type=f32) * HD ** (-0.5)
+            ok = lax.broadcasted_iota(jnp.int32, (256, n), 0) + 256 * i >= lax.broadcasted_iota(jnp.int32, (256, n), 1)
+            s = jnp.where(ok, s, -1e30)
+            p = jnp.exp(s - jnp.max(s, axis=1, keepdims=True))
+            total = jnp.sum(p, axis=1, keepdims=True)
+            m = jnp.dot(p.astype(bf), values[:n], preferred_element_type=f32)
+            out[rows, hs] = (m / total).astype(bf)
+
+
+def attention(q, kv):
+    V = pl.BlockSpec(memory_space=pltpu.VMEM)
+    return pl.pallas_call(
+        attention_kernel,
+        out_shape=jax.ShapeDtypeStruct((1024, 256), jnp.bfloat16),
+        in_specs=[V, V],
+        out_specs=V,
+        compiler_params=pltpu.CompilerParams(vmem_limit_bytes=60000000),
+        name="attention",
+    )(q, kv)
+
+
 def shards(
     patches,
     window_ids,
@@ -369,74 +617,13 @@
     merged_rows = vision_block(
         patches, window_ids, vit_norm, vit_qkv_w, vit_qkv_b, vit_out_w, merge_norm
     )
-    own_index = lax.axis_index("mp")
     merged = merged_rows
     m, kvt, kvb, info = prepared(merged, owner, slot_of_row, kv_w, kv_b)
     part, wq, wkv, kb, info_all = merger(
         m, merge_w1.T, merge_b1[:, None], merge_w2, merge_b2[None], q_w, kvt, kvb, info
     )
-    embedded = lax.all_to_all(
-        part.reshape(4, 32, 2048), "mp", 0, 0, tiled=True,
-        axis_index_groups=[[4 * i + j for j in range(4)] for i in range(4)],
-    ).transpose(1, 0, 2).reshape(32, 8192)
-    seq_rows = text_embeds.shape[0]
-    groups = lax.axis_size("dp")
-    capacity = seq_rows // groups
-    target_group = owner[:, 0]
-    onehot = (target_group[:, None] == jnp.arange(groups, dtype=jnp.int32)[None, :]).astype(
-        jnp.int32
-    )
-    rank_in = jnp.sum((jnp.cumsum(onehot, axis=0) - onehot) * onehot, axis=1)
-    send_slot = target_group * capacity + rank_in
-    selector = send_slot[None, :] == jnp.arange(seq_rows, dtype=jnp.int32)[:, None]
-    buffer = jnp.dot(
-        selector.astype(jnp.bfloat16), embedded, preferred_element_type=jnp.float32
-    ).astype(jnp.bfloat16)
-    buffer = buffer.reshape(groups, capacity, embedded.shape[1])
-    marks = jnp.sum(selector.astype(jnp.int32), axis=1).reshape(groups, capacity)
-    arrived, arrived_marks = (
-        lax.all_to_all(buffer, "dp", split_axis=0, concat_axis=0, tiled=True),
-        lax.all_to_all(marks, "dp", split_axis=0, concat_axis=0, tiled=True),
-    )
-    arrived = arrived.reshape(seq_rows, embedded.shape[1])
-    arrived_marks = arrived_marks.reshape(seq_rows)
-    chosen = slot_of_row[0]
-    sequence = jnp.where(arrived_marks[chosen][:, None] > 0, arrived[chosen], text_embeds)
-    llm_normed = rms_norm(sequence, llm_norm).astype(jnp.bfloat16)
-    query_cols = q_w.shape[1]
-    kv_cols = kv_w.shape[2]
-    shard_rows = lax.all_gather(llm_normed, "mp", axis=0, tiled=True)
-    projected = jnp.concatenate(
-        [
-            jnp.dot(shard_rows, q_w, preferred_element_type=jnp.float32),
-            jnp.dot(shard_rows, kv_w[0], preferred_element_type=jnp.float32),
-            jnp.dot(shard_rows, kv_w[1], preferred_element_type=jnp.float32),
-        ],
-        axis=1,
-    )
-    length = projected.shape[0]
-    queries = (projected[:, :query_cols] + q_b).astype(jnp.bfloat16)
-    key_rows = (projected[:, query_cols : query_cols + kv_cols] + kv_b[0]).astype(jnp.bfloat16)
-    value_rows = (projected[:, query_cols + kv_cols :] + kv_b[1]).astype(jnp.bfloat16)
-    stacked = jnp.stack([key_rows.T, value_rows.T])
-    all_heads = gathered_copies(stacked, "mp", 1)
-    heads_here = query_cols // HD
-    group_size = QH // KVH
-    kv_head = own_index * heads_here // group_size
-    by_head = all_heads.reshape(2, HD, KVH, length)
-    key_cols = lax.dynamic_index_in_dim(by_head[0], kv_head, 1, keepdims=False)
-    value_cols = lax.dynamic_index_in_dim(by_head[1], kv_head, 1, keepdims=False)
-    query_heads = queries.reshape(length, heads_here, HD)
-    scores = jnp.einsum(
-        "qhd,dk->hqk", query_heads, key_cols, preferred_element_type=jnp.float32
-    ) * HD ** (-0.5)
-    allowed = jnp.arange(length)[:, None] >= jnp.arange(length)[None, :]
-    scores = jnp.where(allowed[None], scores, -1e30)
-    peak = jnp.max(scores, axis=-1, keepdims=True)
-    weights = jnp.exp(scores - peak)
-    weights = (weights / jnp.sum(weights, axis=-1, keepdims=True)).astype(jnp.bfloat16)
-    mixture = jnp.einsum("hqk,dk->qhd", weights, value_cols, preferred_element_type=jnp.float32)
-    return mixture.astype(jnp.bfloat16).reshape(length, query_cols)
+    q, kv = language(part, info_all, wq, wkv, kb, text_embeds, llm_norm[None], q_b[None])
+    return attention(q, kv)
 
 
 def solution(mesh):

time: 345 us -> 182 us (0.53)
  waiting for transfers between devices: 151 us -> 0 us
  Pallas kernels: 89.3 us -> 166 us
  matrix products: 47 us -> 4.93 us
  starting transfers between devices: 16.3 us -> 0 us
  between operations: 13.7 us -> 0.15 us
  local copies, waits for them, and re-layouts: 17.7 us -> 8.65 us
  other arithmetic: 9.03 us -> 2.19 us
    all_gather x1 -> x0, waiting for transfers between devices: 107 us -> none  [shards(): shard_rows = lax.all_gather(llm_normed, 'mp', axis=0, tiled=True)]
    pallas_call x0 -> x2, Pallas kernels: none -> 76.4 us  [the longest x1 70.8 us: language(): pl.pallas_call(language_kernel, out_shape=(S((1024, 256), bf), S((1024, 2...]
    all_to_all x4 -> x0, waiting for transfers between devices: 44.1 us -> none  [the longest x1 20 us: copy_for_each(): lax.all_to_all(jnp.broadcast_to(x[None], (size, *x.shape)), axis, 0, 0, t...]
    dot_general x5 -> x0, matrix products: 31.8 us -> none  [the longest x1 10.9 us: shards(): jnp.dot(shard_rows, kv_w[1], preferred_element_type=jnp.float32)]
    all_to_all x4 -> x0, starting transfers between devices: 16.1 us -> none  [the longest x1 5.32 us: copy_for_each(): lax.all_to_all(jnp.broadcast_to(x[None], (size, *x.shape)), axis, 0, 0, t...]
    sub x1 -> x0, matrix products: 6.56 us -> none  [shards(): weights = jnp.exp(scores - peak)]
  transfers between devices with their start and end apart: 5 -> 0, of which waited for: 5 -> 0; matrix products, arithmetic and copies ran while one was open for 4% -> 0% of each run, Pallas kernels for 0% -> 0%
where the time goes in v2:
time: 182 us
  Pallas kernels  166 us (91%)
  local copies, waits for them, and re-layouts  8.65 us (5%)
  matrix products  4.93 us (3%)
  other arithmetic  2.19 us (1%)
    pallas_call x1, Pallas kernels, merger(): pl.pallas_call(merger_kernel, out_shape=(S((128, 2048), bf), S((4, 2048,...  89.4 us
    pallas_call x1, Pallas kernels, language(): pl.pallas_call(language_kernel, out_shape=(S((1024, 256), bf), S((1024, 2...  70.8 us
    pallas_call x1, Pallas kernels, attention(): pl.pallas_call(attention_kernel, out_shape=jax.ShapeDtypeStruct((1024, 25...  5.61 us

profile of v2, /device:TPU:0, one launch (start us, length us, event | category | flops | bytes accessed | tf_op | source)
XLA Modules:
  0.0 181.7 jit_solution(8456083340940723378)
XLA Ops:
  0.0 0.0 copy-start
  0.0 1.2 fusion.7
  1.3 0.8 dynamic_update_slice.6
  2.0 0.8 dynamic_update_slice.7.info
  2.8 0.0 copy-start.2
  2.8 0.8 reshape.122
  3.6 0.1 copy.33
  3.7 0.6 pad.4.kvb
  4.3 0.8 broadcast_compare_fusion
  5.1 1.5 broadcast_in_dim.43.b1
  6.6 3.5 %fusion.3 = bf16[128,1920]{1,0:T(8,128)(2,1)S(1)} fusion(bf16[1280,1920]{1,0:T(8,128)(2,1)} %param.25, f32[1920]{0:T(1024)} %param.26, bf16[128,1280]{1,0:T(8,128)(2,1)} %param.19, f32[1280]{0:T(1024)} %param.24, f32[128]{0:T(128)S(1)} %add_rsqrt_fusion.1), kind=kOutput, calls=%fused_computation.5 | convolution fusion | flops 630292480 | bytes 5747712 | tf_op jit(solution)/shard_map/dot_general | solution.py:39
  10.0 0.0 copy-start.1
  10.0 0.0 copy-start.3
  10.1 0.3 copy.26
  10.3 0.4 fusion.16
  10.7 0.3 fusion.6
  11.0 0.0 copy-done.2
  11.0 0.3 convolution_convert_fusion
  11.3 0.0 copy-done
  11.3 0.0 copy-done.1
  11.3 0.5 multiply_reduce_fusion
  11.9 0.0 copy-done.3
  11.9 0.1 multiply_convert_fusion
  12.0 0.1 reshape.119
  12.1 0.8 copy.37
  12.8 1.5 reshape.120
  14.3 1.6 copy.36
  15.9 89.4 %merger.1 = (bf16[128,2048]{1,0:T(8,128)(2,1)}, bf16[4,2048,256]{2,1,0:T(8,128)(2,1)}, bf16[4,4,16,2048]{3,2,1,0:T(8,128)(2,1)}, f32[4,4,8,128]{3,2,1,0:T(8,128)}, s32[4,8,128]{2,1,0:T(8,128)}) custom-call(bf16[4,32,1280]{2,1,0:T(8,128)(2,1)} %bitcast.50, bf16[320,5120]{1,0:T(8,128)(2,1)} %bitcast.46, f32[320,1]{1,0:T(8,128)} %broadcast_in_dim.43.b1, ...), custom_call_target="tpu_custom_call" | custom-call | tf_op jit(solution)/shard_map/merger/pallas_call | solution.py:310
  105.3 70.8 %language.1 = (bf16[1024,256]{1,0:T(8,128)(2,1)}, bf16[1024,256]{1,0:T(8,128)(2,1)}) custom-call(bf16[128,2048]{1,0:T(8,128)(2,1)} %get-tuple-element.12.part, s32[4,8,128]{2,1,0:T(8,128)} %get-tuple-element.13.info, bf16[4,2048,256]{2,1,0:T(8,128)(2,1)} %get-tuple-element.14.wq, bf16[4,4,16,2048]{3,2,1,0:T(8,128)(2,1)} %get-tuple-element.15.wkv, ...), custom_call_target="tpu_custom_call" | custom-call | tf_op jit(solution)/shard_map/language/pallas_call | solution.py:534
  176.1 5.6 %attention.1 = bf16[1024,256]{1,0:T(8,128)(2,1)} custom-call(bf16[1024,256]{1,0:T(8,128)(2,1)} %get-tuple-element.17.q, bf16[1024,256]{1,0:T(8,128)(2,1)} %get-tuple-element.18.kv), custom_call_target="tpu_custom_call" | custom-call | tf_op jit(solution)/shard_map/attention/pallas_call | solution.py:586
  (3 shorter events, 0.0 us)
Async XLA Ops:
  0.0 11.3 %copy-start = (bf16[640,1280]{1,0:T(8,128)(2,1)S(1)}, bf16[640,1280]{1,0:T(8,128)(2,1)}, u32[]{:S(2)}) copy-start(bf16[640,1280]{1,0:T(8,128)(2,1)} %param.27) | copy-start | bytes 4915204
  2.8 8.2 %copy-start.2 = (s32[8,128]{1,0:T(8,128)}, s32[8,128]{1,0:T(8,128)S(1)}, u32[]{:S(2)}) copy-start(s32[8,128]{1,0:T(8,128)S(1)} %dynamic_update_slice.7.info) | copy-start | bytes 12292
  10.0 1.3 copy-start.1
  10.0 1.8 %copy-start.3 = (f32[1280]{0:T(1024)S(1)}, f32[1280]{0:T(1024)}, u32[]{:S(2)}) copy-start(f32[1280]{0:T(1024)} %param.28) | copy-start | bytes 15364

commit v3 on v1

v3 whole, which is shorter than its diff:
```python
import jax
import jax.numpy as jnp
from jax import lax
from jax.experimental import pallas as pl
from jax.experimental.pallas import tpu as pltpu
from jax.sharding import PartitionSpec as P

VHD = 80
HD = 128
MESH = pl.DeviceIdType.MESH
NT = (((1,), (1,)), ((), ()))


class Copies:
    def __init__(self, send, recv, local):
        self.send, self.recv, self.local = send, recv, local
        self.n, self.m = 0, 0
        self.sent = []

    def remote(self, src, dst, dev):
        k = self.n
        self.n += 1
        c = pltpu.make_async_remote_copy(
            src_ref=src, dst_ref=dst, send_sem=self.send.at[k], recv_sem=self.recv.at[k],
            device_id=dev, device_id_type=MESH)
        c.start()
        self.sent.append(c)
        return c

    def here(self, src, dst):
        k = self.m
        self.m += 1
        c = pltpu.make_async_copy(src, dst, self.local.at[k])
        c.start()
        return c

    def drain(self):
        for c in self.sent:
            c.wait_send()
        self.sent = []


def places():
    mp, dp = lax.axis_index("mp"), lax.axis_index("dp")
    y, x = mp // 4, lax.rem(mp, 4)
    X = lambda s: (dp, y * 4 + lax.rem(x + s + 4, 4))
    Y = lambda s: (dp, lax.rem(y + s + 4, 4) * 4 + x)
    Z = lambda s: (lax.rem(dp + 2 * s + 8, 8), mp)
    other = (dp + 1 - 2 * lax.rem(dp, 2), mp)
    return dp, y, x, X, Y, Z, other


def meet(devs):
    barrier = pltpu.get_barrier_semaphore()
    for d in devs:
        pl.semaphore_signal(barrier, inc=1, device_id=d, device_id_type=MESH)
    pl.semaphore_wait(barrier, len(devs))


N3 = 300


def vision(patches, ids, norm, qkv_w, qkv_b, out_w, gain):
    bf, f32 = jnp.bfloat16, jnp.float32
    iota = lambda shape, d: lax.broadcasted_iota(jnp.int32, shape, d)
    i, s = iota((128, 128), 0), iota((128, 128), 1)
    perm = (s == (i % 32) * 4 + i // 32).astype(f32).astype(bf)
    p = jnp.dot(perm, patches[...], preferred_element_type=f32)
    wide = jnp.broadcast_to(ids[...].astype(f32), (128, 128)).astype(bf)
    across = lax.dot_general(wide, perm, NT, preferred_element_type=f32)
    same = across == across.T
    normed = p * lax.rsqrt(jnp.mean(p * p, axis=1, keepdims=True) + 1e-6) * norm[...]
    qkv = (jnp.dot(normed.astype(bf), qkv_w[...], preferred_element_type=f32) + qkv_b[...]).astype(bf)
    tiles = [None] * 5
    for h in range(8):
        lo, hi = 80 * h // 128, (80 * h + 207) // 128
        lane = iota((128, 128 * (hi - lo)), 1) + 128 * lo
        here = (lane >= 80 * h) & (lane < 80 * h + 80)
        part = lambda k: qkv[:, 640 * k + 128 * lo:640 * k + 128 * hi]
        zero = jnp.zeros((), bf)
        sc = lax.dot_general(jnp.where(here, part(0), zero), part(1), NT, preferred_element_type=f32) * VHD ** (-0.5)
        sc = jnp.where(same, sc, -1e30)
        e = jnp.exp(sc - jnp.max(sc, axis=1, keepdims=True))
        w = (e / jnp.sum(e, axis=1, keepdims=True)).astype(bf)
        mix = jnp.dot(w, jnp.where(here, part(2), zero), preferred_element_type=f32)
        for t in range(lo, hi):
            v = mix[:, 128 * (t - lo):128 * (t - lo + 1)]
            tiles[t] = v if tiles[t] is None else tiles[t] + v
    mixed = jnp.concatenate(tiles, axis=1).astype(bf)
    r = (p + jnp.dot(mixed, out_w[...], preferred_element_type=f32)).astype(bf).astype(f32)
    return (r * lax.rsqrt(jnp.mean(r * r, axis=1, keepdims=True) + 1e-6) * gain[...]).astype(bf)


def whole_kernel(patches, ids, owner, slots, text, vnorm, qkv_w, qkv_b, out_w, mnorm, w1, b1, w2, b2, gain, qw, qb,
                 kvw, kvb, q_out, kv_out,
                 MS, G, QKVW, OUTW, w1v, H, HT, W2, wq, wkv, KVS, KVX, KBS, kb, INS, info, RW, RQ,
                 PC, RO, RN, T, TR, SB, R, A, SS, SY, SC, Q0, QR, QL, QO, RQO, RQN, KP, RKV, send, recv, local):
    dp, y, x, X, Y, Z, other = places()
    md = lambda v, s: lax.rem(v + s + 4, 4)
    bf, f32 = jnp.bfloat16, jnp.float32
    iota = lambda shape, d: lax.broadcasted_iota(jnp.int32, shape, d)
    e, mp = dp, y * 4 + x
    cp = Copies(send, recv, local)
    lv = [cp.here(qkv_w, QKVW), cp.here(out_w, OUTW), cp.here(w1, w1v)]
    group = [(lax.rem(dp + s, 8), mp) for s in (2, 6, 1, 3, 5, 7, 4)]
    meet([X(1), X(2), X(3), Y(1), Y(2), Y(3)] + group)
    A2, B2 = pl.ds(0, 2), pl.ds(2, 2)
    cols = lambda xd: pl.ds(pl.multiple_of(2048 * xd + 256 * e, 256), 256)
    mine = pl.ds(pl.multiple_of(256 * e, 256), 256)
    first, second = pl.ds(0, 2), pl.ds(2, 2)

    xo = md(x, 2)
    w2_half = [pl.ds(0, 160), pl.ds(160, 160)]
    q_half = lambda v, i: pl.ds(pl.multiple_of(2048 * v + 256 * e + 128 * i, 128), 128)
    w2r = [cp.remote(w2.at[w2_half[i], cols(xo)], RW.at[i], X(1 - 2 * i)) for i in range(2)]
    w2d = [cp.remote(w2.at[:, cols(md(x, s))], W2.at[x, :, mine], X(s)) for s in (1, -1)]
    qr = [cp.remote(qw.at[q_half(xo, i), :], RQ.at[i], X(1 - 2 * i)) for i in range(2)]
    qd = [cp.remote(qw.at[cols(md(x, s)), :], wq.at[x, mine, :], X(s)) for s in (1, -1)]
    wl = [cp.here(w2.at[:, cols(x)], W2.at[x, :, mine]), cp.here(qw.at[cols(x), :], wq.at[x, mine, :])]

    lv[0].wait()
    lv[1].wait()
    MS[...] = vision(patches, ids, vnorm, QKVW, qkv_b, OUTW, mnorm).reshape(4, 32, 1280)

    a1 = {s: cp.remote(MS.at[A2], G.at[A2, y, x], X(s)) for s in (1, -1)}
    c1 = {s: cp.remote(MS.at[B2], G.at[B2, y, x], Y(s)) for s in (1, -1)}
    a2 = {(0, s): cp.remote(MS.at[A2], G.at[A2, y, x], Y(s)) for s in (1, -1)}
    c2 = {(0, s): cp.remote(MS.at[B2], G.at[B2, y, x], X(s)) for s in (1, -1)}
    gl = cp.here(MS, G.at[:, y, x])
    for c in w2r:
        c.wait_recv()
    w2f = [cp.remote(RW.at[i], W2.at[md(x, 2 * i - 1), w2_half[i], mine], X(1 - 2 * i)) for i in range(2)]
    for c in w2d:
        c.wait_recv()

    i64, s64 = iota((64, 64), 0), iota((64, 64), 1)
    order = (s64 == (i64 // 8 % 2) * 32 + (i64 % 8) * 4 + i64 // 16).astype(f32).astype(bf)
    for n in range(4):
        cs = slice(2048 * n, 2048 * (n + 1))
        v = jnp.dot(order, kvw[:, :, cs].reshape(64, 2048), preferred_element_type=f32)
        KVS[:, :, cs] = v.astype(bf).reshape(4, 16, 2048)
    li, ll = iota((128, 128), 0), iota((128, 128), 1)
    rows = []
    flat = jnp.concatenate([kvb[0:1, :], kvb[1:2, :], jnp.zeros((1, 64), f32)], axis=1)
    down = jnp.broadcast_to(flat, (128, 128)).T
    for j in range(4):
        keep = (li == (ll // 8) * 32 + (ll % 8) * 4 + j) & (ll < 16)
        rows.append(jnp.sum(jnp.where(keep, down, 0.0), axis=0, keepdims=True))
    KBS[...] = jnp.concatenate(rows + [jnp.zeros((4, 128), f32)], axis=0)
    own4 = jnp.broadcast_to(jnp.concatenate([owner[...]] * 4, axis=1), (8, 128))
    slot2 = jnp.broadcast_to(jnp.concatenate([slots[...]] * 2, axis=1), (8, 128))
    t0, t1 = iota((8, 128), 0), iota((8, 128), 1)
    INS[...] = jnp.where((t0 == 0) & (t1 // 32 == x), own4,
                         jnp.where((t0 == 1 + x // 2) & (t1 // 64 == x % 2), slot2, 0))
    wx = []
    for s in (1, 3, 2):
        wx.append(cp.remote(KVS.at[:, :, cols(md(x, s))], KVX.at[x], X(s)))
        wx.append(cp.remote(KBS, kb.at[y, x], X(s)))
        wx.append(cp.remote(INS, info.at[x], X(s)))
    KVX[x] = KVS[:, :, cols(x)]
    kb[y, x] = KBS[...]
    info[x] = INS[...]

    af, cf = {}, {}
    for s in (1, -1):
        a1[s].wait_recv()
        xs, j = md(x, -s), 0 if s == 1 else 1
        af[s] = cp.remote(G.at[j, y, xs], G.at[j, y, xs], X(s))
        for t in (1, -1):
            a2[(-s, t)] = cp.remote(G.at[A2, y, xs], G.at[A2, y, xs], Y(t))
        c1[s].wait_recv()
        ys, j = md(y, -s), 2 if s == 1 else 3
        cf[s] = cp.remote(G.at[j, ys, x], G.at[j, ys, x], Y(s))
        for t in (1, -1):
            c2[(-s, t)] = cp.remote(G.at[B2, ys, x], G.at[B2, ys, x], X(t))
    last = []

    def pass_on(p):
        for t in (1, -1):
            a2[(p, t)].wait_recv()
            xs, ys, j = md(x, p), md(y, -t), 0 if t == 1 else 1
            last.append(cp.remote(G.at[j, ys, xs], G.at[j, ys, xs], Y(t)))
            c2[(p, t)].wait_recv()
            ys, xs, j = md(y, p), md(x, -t), 2 if t == 1 else 3
            last.append(cp.remote(G.at[j, ys, xs], G.at[j, ys, xs], X(t)))

    pass_on(0)
    bands = lambda r: pl.ds(pl.multiple_of(256 * r, 256), 256)

    def piece(name, r, half=None):
        h = pl.ds(0, 4) if half is None else (first, second)[half]
        if name == "w2":
            return W2.at[h, :, bands(r)]
        if name == "q":
            return wq.at[h, bands(r), :]
        return wkv.at[h, :, :, bands(r)]

    zs, ds_, zf = {}, {}, {}

    def z_start(name):
        zs[name] = {s: cp.remote(piece(name, e), piece(name, e), Z(s)) for s in (1, -1)}
        ds_[name] = [cp.remote(piece(name, e), piece(name, e), other)]

    def z_mid(name):
        zf[name] = {}
        for s in (1, -1):
            zs[name][s].wait_recv()
            r, h = lax.rem(e - 2 * s + 8, 8), 0 if s == 1 else 1
            zf[name][s] = cp.remote(piece(name, r, h), piece(name, r, h), Z(s))
            ds_[name].append(cp.remote(piece(name, r), piece(name, r), other))

    def z_end(name):
        for s in (1, -1):
            zf[name][s].wait_recv()
        r = lax.rem(e + 4, 8)
        ds_[name].append(cp.remote(piece(name, r), piece(name, r), other))

    def z_all(name):
        for c in ds_[name]:
            c.wait_recv()

    for c in w2f:
        c.wait_recv()
    wl[0].wait()
    z_start("w2")
    for c in qr:
        c.wait_recv()
    qf = [cp.remote(RQ.at[i], wq.at[md(x, 2 * i - 1), pl.ds(pl.multiple_of(256 * e + 128 * i, 128), 128), :],
                    X(1 - 2 * i)) for i in range(2)]
    for c in wx:
        c.wait_recv()
    ky = []
    for s in (1, 2, 3):
        yd = md(y, s)
        ky.append(cp.remote(KVX.at[:, yd], wkv.at[y, :, :, mine], Y(s)))
        ky.append(cp.remote(kb.at[y], kb.at[y], Y(s)))
    wkv[y, :, :, mine] = KVX[:, y]
    for s in (1, -1):
        af[s].wait_recv()
        cf[s].wait_recv()
    xf, yf = md(x, 2), md(y, 2)
    for t in (1, -1):
        a2[(2, t)] = cp.remote(G.at[A2, y, xf], G.at[A2, y, xf], Y(t))
        c2[(2, t)] = cp.remote(G.at[B2, yf, x], G.at[B2, yf, x], X(t))
    pass_on(-1)
    pass_on(1)
    for c in qd + qf:
        c.wait_recv()
    wl[1].wait()
    z_mid("w2")
    z_start("q")
    for c in ky:
        c.wait_recv()
    z_start("kv")
    pass_on(2)
    for c in last:
        c.wait_recv()
    gl.wait()
    lv[2].wait()
    wide = jnp.concatenate([b1[...], jnp.zeros((1, 64), f32)], axis=1)
    bcol = jnp.broadcast_to(wide, (128, 384)).T[0:320, :]
    bcol = jnp.concatenate([bcol, bcol], axis=1)
    for g in range(2):
        acc = None
        for j in range(4):
            p = lax.dot_general(w1v[:, 1280 * j:1280 * (j + 1)], G[j, 2 * g:2 * g + 2].reshape(256, 1280), NT,
                                preferred_element_type=f32)
            acc = p if acc is None else acc + p
        v = acc + bcol
        v = 0.5 * v * (1.0 + lax.erf(v * (0.5 ** 0.5)))
        H[x, :, 256 * g:256 * (g + 1)] = v.astype(bf)
    h1 = {s: cp.remote(H.at[x], H.at[x], X(s)) for s in (1, -1)}
    z_end("w2")
    z_mid("q")
    z_mid("kv")
    h2 = []
    for s in (1, -1):
        h1[s].wait_recv()
        xs, r = md(x, -s), pl.ds(0, 160) if s == 1 else pl.ds(160, 160)
        h2.append(cp.remote(H.at[xs, r, :], H.at[xs, r, :], X(s)))
    quarter = lambda v: pl.ds(pl.multiple_of(2048 * v, 2048), 2048)
    th = [pl.ds(0, 32), pl.ds(32, 32)]
    tr = [cp.remote(text.at[th[i], quarter(xo)], TR.at[i], X(1 - 2 * i)) for i in range(2)]
    td = [cp.remote(text.at[:, quarter(md(x, s))], T.at[x], X(s)) for s in (1, -1)]
    tl = cp.here(text.at[:, quarter(x)], T.at[x])
    tab = info[0] + info[1] + info[2] + info[3]
    own = tab[0:1, :]
    down = jnp.broadcast_to(own.astype(f32), (128, 128)).T.astype(jnp.int32)
    before = (down == own) & (li < ll) & (li // 32 == ll // 32)
    rank = jnp.sum(before.astype(jnp.int32), axis=0, keepdims=True)
    target = own * 32 + (iota((1, 128), 1) // 32) * 8 + rank
    pick = (iota((256, 128), 0) == target).astype(f32).astype(bf)
    choose = []
    for i in range(2):
        s = jnp.broadcast_to(tab[1 + i:2 + i, :].astype(f32), (128, 128)).T.astype(jnp.int32)
        s = jnp.concatenate([s, s], axis=1)
        lane, row = iota((128, 256), 1), iota((128, 256), 0)
        hit = ((lane // 32) * 8 + lane % 8 == s) & ((lane % 32) // 8 == row // 64 + 2 * i)
        choose.append(hit.astype(f32).astype(bf))
    z_all("w2")
    for c in h2:
        c.wait_recv()
    HT[...] = H[...].reshape(1280, 512).T

    lo, hi = pl.ds(0, 64), pl.ds(64, 64)
    yr, yl = md(y, 1), md(y, -1)
    ro, rn, hand, handl = {}, {}, {}, {}

    def mul(c):
        cs = slice(512 * c, 512 * (c + 1))
        v = jnp.dot(HT[...], W2[:, :, cs].reshape(1280, 512), preferred_element_type=f32)
        PC[c] = v.astype(bf).reshape(4, 128, 512)
        ro[c] = [cp.remote(PC.at[c, md(y, 2), lo], RO.at[c, 0], Y(1)),
                 cp.remote(PC.at[c, md(y, 2), hi], RO.at[c, 1], Y(-1))]
        rn[c] = [cp.remote(PC.at[c, yr, hi], RN.at[c, 0, hi], Y(1)),
                 cp.remote(PC.at[c, yl, lo], RN.at[c, 1, lo], Y(-1))]

    def relay_y(c):
        ro[c][0].wait_recv()
        PC[c, yr, 0:64, :] = (PC[c, yr, 0:64, :].astype(f32) + RO[c, 0].astype(f32)).astype(bf)
        rn[c].append(cp.remote(PC.at[c, yr, lo], RN.at[c, 0, lo], Y(1)))
        ro[c][1].wait_recv()
        PC[c, yl, 64:128, :] = (PC[c, yl, 64:128, :].astype(f32) + RO[c, 1].astype(f32)).astype(bf)
        rn[c].append(cp.remote(PC.at[c, yl, hi], RN.at[c, 1, hi], Y(-1)))

    def give(c):
        for k in rn[c]:
            k.wait_recv()
        v = PC[c, y].astype(f32) + RN[c, 0].astype(f32) + RN[c, 1].astype(f32)
        v = (v + b2[:, pl.ds(pl.multiple_of(2048 * x + 512 * c, 512), 512)]).astype(bf)
        SB[c, :, :, 0:512] = jnp.dot(pick, v, preferred_element_type=f32).astype(bf).reshape(8, 32, 512)
        w = pl.ds(0, 512)
        if c == 0:
            v = jnp.dot(pick, jnp.ones((128, 128), bf), preferred_element_type=f32)
            SB[c, :, :, 512:640] = v.astype(bf).reshape(8, 32, 128)
            w = pl.ds(0, 640)
        hand[c] = [cp.remote(SB.at[c, d[0], :, w], R.at[c, dp, :, w], d) for d in group]
        handl[c] = cp.here(SB.at[c, dp, :, w], R.at[c, dp, :, w])

    h = [pl.ds(0, 128), pl.ds(128, 128)]
    gx = gain[:, quarter(x)]
    filled, sq, yc = [None, None], [None, None], {1: [], -1: []}

    def take(c):
        cs = slice(512 * c, 512 * (c + 1))
        for k in hand[c]:
            k.wait_recv()
        handl[c].wait()
        for i in range(2):
            if c == 0:
                seen = jnp.dot(choose[i], R[0, :, :, 512:640].reshape(256, 128), preferred_element_type=f32)
                filled[i] = seen[:, 0:1] > 0.5
            v = jnp.dot(choose[i], R[c, :, :, 0:512].reshape(256, 512), preferred_element_type=f32)
            v = jnp.where(filled[i], v, T[2 * i:2 * i + 2, :, cs].reshape(128, 512).astype(f32))
            t = jnp.sum(v * v, axis=1, keepdims=True)
            sq[i] = t if c == 0 else sq[i] + t
            A[y, 128 * i:128 * (i + 1), cs] = (v * gx[:, cs]).astype(bf)
            w, s = pl.ds(512 * c, 512), 1 - 2 * i
            yc[s].append(cp.remote(A.at[y, h[i], w], A.at[y, h[i], w], Y(s)))

    mul(0)
    mul(1)
    mul(2)
    relay_y(0)
    mul(3)
    relay_y(1)
    give(0)
    for c in tr:
        c.wait_recv()
    tf = [cp.remote(TR.at[i], T.at[md(x, 2 * i - 1), th[i]], X(1 - 2 * i)) for i in range(2)]
    relay_y(2)
    give(1)
    relay_y(3)
    z_end("q")
    z_end("kv")
    for c in td + tf:
        c.wait_recv()
    tl.wait()
    take(0)
    give(2)
    take(1)
    give(3)
    take(2)
    take(3)
    yo = {1: cp.remote(A.at[y, h[1]], A.at[y, h[1]], Y(1)), -1: cp.remote(A.at[y, h[0]], A.at[y, h[0]], Y(-1))}
    SS[x] = jnp.concatenate([jnp.broadcast_to(t, (128, 128)).T[0:8, :] for t in sq], axis=1)
    sx = [cp.remote(SS.at[x], SS.at[x], X(s)) for s in (1, 2, 3)]
    z_all("q")
    z_all("kv")

    def pair(ga, ia, gb, ib):
        a = jnp.concatenate([A[ga, 128 * ia:128 * (ia + 1), :], A[gb, 128 * ib:128 * (ib + 1), :]], axis=0)
        us = []
        for g, i in ((ga, ia), (gb, ib)):
            at = lambda off, n, g=g, i=i: pl.ds(pl.multiple_of(256 * g + 128 * i + off, n), n)
            us.append(dict(g=g, i=i, rows=at(0, 128), lo=at(0, 64), hi=at(64, 64), slot=2 * g + i, at=at))
        prod = lambda s: jnp.dot(a, wq[md(x, s)], preferred_element_type=f32)

        def put(ref, v):
            v = v.astype(ref.dtype)
            for n, u in enumerate(us):
                ref[u["rows"], :] = v[128 * n:128 * (n + 1)]

        put(QO, prod(2))
        for u in us:
            u["o"] = [cp.remote(QO.at[u["lo"]], RQO.at[0, u["lo"]], X(1)),
                      cp.remote(QO.at[u["hi"]], RQO.at[1, u["hi"]], X(-1))]
        put(KP, lax.dot_general(a, wkv[...].reshape(256, 2048), NT, preferred_element_type=f32))
        for u in us:
            u["k"] = []
            for s in (2, 1, 3):
                xd = md(x, s)
                src = pl.ds(pl.multiple_of(256 * u["g"] + 128 * u["i"] + 32 * xd, 32), 32)
                u["k"].append(cp.remote(KP.at[src], RKV.at[x, u["slot"]], X(s)))
        put(QR, prod(1))
        for u in us:
            u["n"] = [cp.remote(QR.at[u["hi"]], RQN.at[0, u["hi"]], X(1))]
        put(QL, prod(-1))
        for u in us:
            u["n"].append(cp.remote(QL.at[u["lo"]], RQN.at[1, u["lo"]], X(-1)))
        put(Q0, prod(0))
        return us

    def relay(us):
        for u in us:
            lo, hi = u["lo"], u["hi"]
            u["o"][0].wait_recv()
            QR[lo, :] = (QR[lo, :].astype(f32) + RQO[0, lo, :].astype(f32)).astype(bf)
            u["n"].append(cp.remote(QR.at[lo], RQN.at[0, lo], X(1)))
            u["o"][1].wait_recv()
            QL[hi, :] = (QL[hi, :].astype(f32) + RQO[1, hi, :].astype(f32)).astype(bf)
            u["n"].append(cp.remote(QL.at[hi], RQN.at[1, hi], X(-1)))

    bias = jnp.concatenate([kb[p // 4, p % 4, pl.ds(y, 1), 0:16] for p in range(16)], axis=1)

    def keys(us):
        for u in us:
            for c in u["k"]:
                c.wait_recv()
            m = pl.ds(pl.multiple_of(256 * u["g"] + 128 * u["i"] + 32 * x, 32), 32)
            v = KP[m, :].astype(f32)
            for s in (1, 2, 3):
                v = v + RKV[md(x, s), u["slot"]].astype(f32)
            sc = SC[m, :]
            v = v * jnp.concatenate([sc, sc], axis=1) + bias
            kv_out[m, :] = v.astype(bf)
            u["f"] = [cp.remote(kv_out.at[m], kv_out.at[m], X(s)) for s in (2, 1, 3)]

    def scale(g):
        v = lax.rsqrt(SY[g] * (1.0 / 8192.0) + 1e-6)
        for i in range(2):
            SC[pl.ds(pl.multiple_of(256 * g + 128 * i, 128), 128), :] = jnp.broadcast_to(
                v[0:1, 128 * i:128 * (i + 1)], (128, 128)).T

    def finish(us):
        for u in us:
            rows = u["rows"]
            for c in u["n"]:
                c.wait_recv()
            sc = SC[rows, :]
            v = Q0[rows, :] + RQN[0, rows, :].astype(f32) + RQN[1, rows, :].astype(f32)
            q_out[rows, :] = (v * jnp.concatenate([sc, sc], axis=1) + qb[...]).astype(bf)
        for u in us:
            for c in u["f"]:
                c.wait_recv()

    u0 = pair(y, 0, y, 1)
    for c in sx:
        c.wait_recv()
    SY[y] = SS[0] + SS[1] + SS[2] + SS[3]
    sy = [cp.remote(SY.at[y], SY.at[y], Y(s)) for s in (1, 2, 3)]
    scale(y)
    relay(u0)
    keys(u0)
    up, dn, op = yr, yl, md(y, 2)
    far = {}
    for c in yc[1]:
        c.wait_recv()
    far[1] = cp.remote(A.at[dn, h[0]], A.at[dn, h[0]], Y(1))
    for c in yc[-1]:
        c.wait_recv()
    far[-1] = cp.remote(A.at[up, h[1]], A.at[up, h[1]], Y(-1))
    u1 = pair(dn, 0, up, 1)
    for c in sy:
        c.wait_recv()
    for g in (dn, up, op):
        scale(g)
    relay(u1)
    keys(u1)
    finish(u0)
    yo[1].wait_recv()
    yo[-1].wait_recv()
    u2 = pair(dn, 1, up, 0)
    relay(u2)
    keys(u2)
    finish(u1)
    finish(u2)
    far[1].wait_recv()
    far[-1].wait_recv()
    u3 = pair(op, 0, op, 1)
    relay(u3)
    keys(u3)
    finish(u3)
    cp.drain()


def whole(patches, ids, owner, slots, text, vnorm, qkv_w, qkv_b, out_w, mnorm, w1, b1, w2, b2, gain, qw, qb, kvw, kvb):
    bf, f32, i32 = jnp.bfloat16, jnp.float32, jnp.int32
    V, ANY = pl.BlockSpec(memory_space=pltpu.VMEM), pl.BlockSpec(memory_space=pl.ANY)
    S = jax.ShapeDtypeStruct
    M = pltpu.VMEM
    return pl.pallas_call(
        whole_kernel,
        out_shape=(S((1024, 256), bf), S((1024, 256), bf)),
        in_specs=[V, V, V, V, ANY, V, ANY, V, ANY, V, ANY, V, ANY, V, V, ANY, V, V, V],
        out_specs=[V] * 2,
        scratch_shapes=[
            M((4, 32, 1280), bf),
            M((4, 4, 4, 32, 1280), bf),
            M((1280, 1920), bf),
            M((640, 1280), bf),
            M((320, 5120), bf),
            M((4, 320, 512), bf),
            M((512, 1280), bf),
            M((4, 320, 2048), bf),
            M((4, 2048, 256), bf),
            M((4, 4, 16, 2048), bf),
            M((4, 16, 8192), bf),
            M((4, 4, 16, 256), bf),
            M((8, 128), f32),
            M((4, 4, 8, 128), f32),
            M((8, 128), i32),
            M((4, 8, 128), i32),
            M((2, 160, 256), bf),
            M((2, 128, 256), bf),
            M((4, 4, 128, 512), bf),
            M((4, 2, 64, 512), bf),
            M((4, 2, 128, 512), bf),
            M((4, 64, 2048), bf),
            M((2, 32, 2048), bf),
            M((4, 8, 32, 640), bf),
            M((4, 8, 32, 640), bf),
            M((4, 256, 2048), bf),
            M((4, 8, 256), f32),
            M((4, 8, 256), f32),
            M((1024, 128), f32),
            M((1024, 256), f32),
            M((1024, 256), bf),
            M((1024, 256), bf),
            M((1024, 256), bf),
            M((2, 1024, 256), bf),
            M((2, 1024, 256), bf),
            M((1024, 256), bf),
            M((4, 8, 32, 256), bf),
            pltpu.SemaphoreType.DMA((N3,)),
            pltpu.SemaphoreType.DMA((N3,)),
            pltpu.SemaphoreType.DMA((16,)),
        ],
        compiler_params=pltpu.CompilerParams(collective_id=1, has_side_effects=True, vmem_limit_bytes=64000000),
        name="whole",
    )(patches, ids, owner, slots, text, vnorm, qkv_w, qkv_b, out_w, mnorm, w1, b1, w2, b2, gain, qw, qb, kvw, kvb)


def attention_kernel(q, kv, out):
    bf, f32 = jnp.bfloat16, jnp.float32
    c, d = lax.broadcasted_iota(jnp.int32, (256, 128), 0), lax.broadcasted_iota(jnp.int32, (256, 128), 1)
    spot = (d // 8) * 16 + d % 8
    keys = jnp.dot(kv[...], (c == spot).astype(f32).astype(bf), preferred_element_type=f32).astype(bf)
    values = jnp.dot(kv[...], (c == spot + 8).astype(f32).astype(bf), preferred_element_type=f32).astype(bf)
    for i in range(4):
        rows = slice(256 * i, 256 * (i + 1))
        n = 256 * (i + 1)
        for h in range(2):
            hs = slice(128 * h, 128 * (h + 1))
            s = lax.dot_general(q[rows, hs], keys[:n], NT, preferred_element_type=f32) * HD ** (-0.5)
            ok = lax.broadcasted_iota(jnp.int32, (256, n), 0) + 256 * i >= lax.broadcasted_iota(jnp.int32, (256, n), 1)
            s = jnp.where(ok, s, -1e30)
            p = jnp.exp(s - jnp.max(s, axis=1, keepdims=True))
            total = jnp.sum(p, axis=1, keepdims=True)
            m = jnp.dot(p.astype(bf), values[:n], preferred_element_type=f32)
            out[rows, hs] = (m / total).astype(bf)


def attention(q, kv):
    V = pl.BlockSpec(memory_space=pltpu.VMEM)
    return pl.pallas_call(
        attention_kernel,
        out_shape=jax.ShapeDtypeStruct((1024, 256), jnp.bfloat16),
        in_specs=[V, V],
        out_specs=V,
        compiler_params=pltpu.CompilerParams(vmem_limit_bytes=60000000),
        name="attention",
    )(q, kv)


def shards(
    patches,
    window_ids,
    owner,
    slot_of_row,
    text_embeds,
    vit_norm,
    vit_qkv_w,
    vit_qkv_b,
    vit_out_w,
    merge_norm,
    merge_w1,
    merge_b1,
    merge_w2,
    merge_b2,
    llm_norm,
    q_w,
    q_b,
    kv_w,
    kv_b,
):
    q, kv = whole(
        patches, window_ids, owner.reshape(1, 32), slot_of_row, text_embeds, vit_norm[None], vit_qkv_w,
        vit_qkv_b[None], vit_out_w, merge_norm[None], merge_w1.T, merge_b1[None], merge_w2, merge_b2[None],
        llm_norm[None], q_w, q_b[None], kv_w.transpose(0, 2, 1), kv_b,
    )
    return attention(q, kv)


def solution(mesh):
    return jax.shard_map(
        shards,
        mesh=mesh,
        in_specs=(
            P(("dp", "mp"), None),
            P(("dp", "mp"), None),
            P(("dp", "mp"), None),
            P(("dp", "mp"), None),
            P(("dp", "mp"), None),
            P(),
            P(),
            P(),
            P(),
            P(),
            P(None, "mp"),
            P("mp"),
            P("mp", None),
            P(),
            P(),
            P(None, "mp"),
            P("mp"),
            P(None, None, "mp"),
            P(None, "mp"),
        ),
        out_specs=P("dp", "mp"),
        check_vma=False,
    )
```

time: 345 us -> 157 us (0.46)
  waiting for transfers between devices: 151 us -> 0 us
  Pallas kernels: 89.3 us -> 152 us
  matrix products: 47 us -> 0 us
  starting transfers between devices: 16.3 us -> 0 us
  between operations: 13.7 us -> 0.01 us
  local copies, waits for them, and re-layouts: 17.7 us -> 5.13 us
  other arithmetic: 9.03 us -> 0 us
    all_gather x1 -> x0, waiting for transfers between devices: 107 us -> none  [shards(): shard_rows = lax.all_gather(llm_normed, 'mp', axis=0, tiled=True)]
    pallas_call x1 -> x2, Pallas kernels: 89.3 us -> 152 us  [the longest x1 146 us: whole(): pl.pallas_call(whole_kernel, out_shape=(S((1024, 256), bf), S((1024, 256)...]
    all_to_all x4 -> x0, waiting for transfers between devices: 44.1 us -> none  [the longest x1 20 us: copy_for_each(): lax.all_to_all(jnp.broadcast_to(x[None], (size, *x.shape)), axis, 0, 0, t...]
    dot_general x9 -> x0, matrix products: 40 us -> none  [the longest x1 10.9 us: shards(): jnp.dot(shard_rows, kv_w[1], preferred_element_type=jnp.float32)]
    all_to_all x4 -> x0, starting transfers between devices: 16.1 us -> none  [the longest x1 5.32 us: copy_for_each(): lax.all_to_all(jnp.broadcast_to(x[None], (size, *x.shape)), axis, 0, 0, t...]
    sub x2 -> x0, matrix products: 6.94 us -> none  [the longest x1 6.56 us: shards(): weights = jnp.exp(scores - peak)]
    reshape x9 -> x0, local copies, waits for them, and re-layouts: 4.08 us -> none  [the longest x2 1.96 us: prepared(): kv_w.transpose(0, 2, 1).reshape(2, 8, 4, 8192).transpose(2, 0, 1, 3)]
  transfers between devices with their start and end apart: 5 -> 0, of which waited for: 5 -> 0; matrix products, arithmetic and copies ran while one was open for 4% -> 0% of each run, Pallas kernels for 0% -> 0%
where the time goes in v3:
time: 157 us
  Pallas kernels  152 us (97%)
  local copies, waits for them, and re-layouts  5.13 us (3%)
    pallas_call x1, Pallas kernels, whole(): pl.pallas_call(whole_kernel, out_shape=(S((1024, 256), bf), S((1024, 256)...  146 us
    pallas_call x1, Pallas kernels, attention(): pl.pallas_call(attention_kernel, out_shape=jax.ShapeDtypeStruct((1024, 25...  5.34 us

profile of v3, /device:TPU:0, one launch (start us, length us, event | category | flops | bytes accessed | tf_op | source)
XLA Modules:
  0.0 156.7 jit_solution(1919704420526654992)
XLA Ops:
  0.0 1.3 broadcast_in_dim.24.b1
  1.3 1.3 broadcast_in_dim.21.vnorm
  2.5 1.3 broadcast_in_dim.23.mnorm
  3.8 1.3 broadcast_in_dim.22.qkv_b
  5.1 146.3 %whole.1 = (bf16[1024,256]{1,0:T(8,128)(2,1)}, bf16[1024,256]{1,0:T(8,128)(2,1)}) custom-call(bf16[128,1280]{1,0:T(8,128)(2,1)} %patches.1, s32[1,128]{1,0:T(1,128)} %ids.1, s32[1,32]{1,0:T(1,128)} %bitcast.11, s32[1,64]{1,0:T(1,128)} %slots.1, bf16[64,8192]{1,0:T(8,128)(2,1)} %text.1, f32[1,1280]{1,0:T(1,128)} %broadcast_in_dim.21.vnorm, ...), custom_call_target="tpu_custom_call" | custom-call | tf_op jit(solution)/shard_map/whole/pallas_call | solution.py:512
  151.4 5.3 %attention.1 = bf16[1024,256]{1,0:T(8,128)(2,1)} custom-call(bf16[1024,256]{1,0:T(8,128)(2,1)} %get-tuple-element.7.q, bf16[1024,256]{1,0:T(8,128)(2,1)} %get-tuple-element.8.kv), custom_call_target="tpu_custom_call" | custom-call | tf_op jit(solution)/shard_map/attention/pallas_call | solution.py:586

commit v4 on v3

v4 whole, which is shorter than its diff:
```python
import jax
import jax.numpy as jnp
from jax import lax
from jax.experimental import pallas as pl
from jax.experimental.pallas import tpu as pltpu
from jax.sharding import PartitionSpec as P

VHD = 80
HD = 128
MESH = pl.DeviceIdType.MESH
NT = (((1,), (1,)), ((), ()))


class Copies:
    def __init__(self, send, recv, local):
        self.send, self.recv, self.local = send, recv, local
        self.groups, self.views, self.m, self.n = {}, {}, 0, 0
        self.sent = []

    def remote(self, src, dst, dev, group=None):
        single = group is None
        if single:
            self.n += 1
            group = self.n
        k = self.groups.setdefault(group, len(self.groups))
        c = pltpu.make_async_remote_copy(
            src_ref=src, dst_ref=dst, send_sem=self.send.at[k], recv_sem=self.recv.at[k],
            device_id=dev, device_id_type=MESH)
        c.start()
        if single:
            self.sent.append(c)
        return c

    def join(self, group, view):
        k = self.groups[group]
        self.views[k] = view
        pltpu.make_async_copy(view, view, self.recv.at[k]).wait()

    def here(self, src, dst):
        k = self.m
        self.m += 1
        c = pltpu.make_async_copy(src, dst, self.local.at[k])
        c.start()
        return c

    def drain(self):
        for c in self.sent:
            c.wait_send()
        for k, view in self.views.items():
            pltpu.make_async_copy(view, view, self.send.at[k]).wait()
        assert len(self.sent) + len(self.views) == len(self.groups)


def places():
    mp, dp = lax.axis_index("mp"), lax.axis_index("dp")
    y, x = mp // 4, lax.rem(mp, 4)
    X = lambda s: (dp, y * 4 + lax.rem(x + s + 4, 4))
    Y = lambda s: (dp, lax.rem(y + s + 4, 4) * 4 + x)
    Z = lambda s: (lax.rem(dp + 2 * s + 8, 8), mp)
    other = (dp + 1 - 2 * lax.rem(dp, 2), mp)
    return dp, y, x, X, Y, Z, other


def meet(devs):
    barrier = pltpu.get_barrier_semaphore()
    for d in devs:
        pl.semaphore_signal(barrier, inc=1, device_id=d, device_id_type=MESH)
    pl.semaphore_wait(barrier, len(devs))


N3 = 117


def vision(patches, ids, norm, qkv_w, qkv_b, out_w, gain):
    bf, f32 = jnp.bfloat16, jnp.float32
    iota = lambda shape, d: lax.broadcasted_iota(jnp.int32, shape, d)
    i, s = iota((128, 128), 0), iota((128, 128), 1)
    perm = (s == (i % 32) * 4 + i // 32).astype(f32).astype(bf)
    p = jnp.dot(perm, patches[...], preferred_element_type=f32)
    wide = jnp.broadcast_to(ids[...].astype(f32), (128, 128)).astype(bf)
    across = lax.dot_general(wide, perm, NT, preferred_element_type=f32)
    same = across == across.T
    normed = p * lax.rsqrt(jnp.mean(p * p, axis=1, keepdims=True) + 1e-6) * norm[...].reshape(1, 1280)
    qkv = (jnp.dot(normed.astype(bf), qkv_w[...], preferred_element_type=f32) + qkv_b[...].reshape(1, 1920)).astype(bf)
    tiles = [None] * 5
    for h in range(8):
        lo, hi = 80 * h // 128, (80 * h + 207) // 128
        lane = iota((128, 128 * (hi - lo)), 1) + 128 * lo
        here = (lane >= 80 * h) & (lane < 80 * h + 80)
        part = lambda k: qkv[:, 640 * k + 128 * lo:640 * k + 128 * hi]
        zero = jnp.zeros((), bf)
        sc = lax.dot_general(jnp.where(here, part(0), zero), part(1), NT, preferred_element_type=f32) * VHD ** (-0.5)
        sc = jnp.where(same, sc, -1e30)
        e = jnp.exp(sc - jnp.max(sc, axis=1, keepdims=True))
        w = (e / jnp.sum(e, axis=1, keepdims=True)).astype(bf)
        mix = jnp.dot(w, jnp.where(here, part(2), zero), preferred_element_type=f32)
        for t in range(lo, hi):
            v = mix[:, 128 * (t - lo):128 * (t - lo + 1)]
            tiles[t] = v if tiles[t] is None else tiles[t] + v
    mixed = jnp.concatenate(tiles, axis=1).astype(bf)
    r = (p + jnp.dot(mixed, out_w[...], preferred_element_type=f32)).astype(bf).astype(f32)
    return (r * lax.rsqrt(jnp.mean(r * r, axis=1, keepdims=True) + 1e-6) * gain[...].reshape(1, 1280)).astype(bf)


def whole_kernel(patches, ids, owner, slots, text, vnorm, qkv_w, qkv_b, out_w, mnorm, w1, b1, w2, b2, gain, qw, qb,
                 kvw, kvb, q_out, kv_out,
                 MS, G, QKVW, OUTW, w1v, H, HT, W2, wq, wkv, KVS, KVX, KBS, kb, INS, info, RW, RQ,
                 PC, RO, RN, T, TR, SB, R, A, SS, SY, SC, Q0, QR, QL, QO, RQO, RQN, KP, RKV, send, recv, local):
    dp, y, x, X, Y, Z, other = places()
    md = lambda v, s: lax.rem(v + s + 4, 4)
    bf, f32 = jnp.bfloat16, jnp.float32
    iota = lambda shape, d: lax.broadcasted_iota(jnp.int32, shape, d)
    e, mp = dp, y * 4 + x
    cp = Copies(send, recv, local)
    lv = [cp.here(qkv_w, QKVW), cp.here(out_w, OUTW), cp.here(w1, w1v)]
    group = [(lax.rem(dp + s, 8), mp) for s in (2, 6, 1, 3, 5, 7, 4)]
    meet([X(1), X(2), X(3), Y(1), Y(2), Y(3)] + group)
    ca, cb = pl.ds(0, 768), pl.ds(768, 512)
    sa = lambda yy, xx: G.at[:, yy, xx, :, ca]
    sb = lambda yy, xx: G.at[:, yy, xx, :, cb]
    cols = lambda xd: pl.ds(pl.multiple_of(2048 * xd + 256 * e, 256), 256)
    mine = pl.ds(pl.multiple_of(256 * e, 256), 256)
    first, second = pl.ds(0, 2), pl.ds(2, 2)

    xo = md(x, 2)
    w2_half = [pl.ds(0, 160), pl.ds(160, 160)]
    q_half = lambda v, i: pl.ds(pl.multiple_of(2048 * v + 256 * e + 128 * i, 128), 128)
    bands = lambda r: pl.ds(pl.multiple_of(256 * r, 256), 256)
    zw, zwf, dw = {}, {}, []

    def w2_start(s):
        xs = md(x, s)
        src = w2.at[:, cols(x)] if s == 0 else W2.at[xs, :, mine]
        zw[s] = {t: cp.remote(src, W2.at[xs, :, mine], Z(t)) for t in (1, -1)}
        dw.append(cp.remote(src, W2.at[xs, :, mine], other, "dw"))

    def w2_mid(s):
        xs, way = md(x, s), 1 if s in (0, 1) else -1
        for t in (1, -1):
            zw[s][t].wait_recv()
            at = W2.at[xs, :, bands(lax.rem(e - 2 * t + 8, 8))]
            if t == way:
                zwf[s] = cp.remote(at, at, Z(t))
            dw.append(cp.remote(at, at, other, "dw"))

    def w2_end(s):
        zwf[s].wait_recv()
        at = W2.at[md(x, s), :, bands(lax.rem(e + 4, 8))]
        dw.append(cp.remote(at, at, other, "dw"))

    w2r = [cp.remote(w2.at[w2_half[i], cols(xo)], RW.at[i], X(1 - 2 * i)) for i in range(2)]
    w2d = [cp.remote(w2.at[:, cols(md(x, s))], W2.at[x, :, mine], X(s)) for s in (1, -1)]
    w2_start(0)
    wl = [cp.here(w2.at[:, cols(x)], W2.at[x, :, mine]), cp.here(qw.at[cols(x), :], wq.at[x, mine, :])]

    lv[0].wait()
    lv[1].wait()
    MS[...] = vision(patches, ids, vnorm, QKVW, qkv_b, OUTW, mnorm).reshape(4, 32, 1280)

    ma, mb = MS.at[:, :, ca], MS.at[:, :, cb]
    a1 = {s: cp.remote(ma, sa(y, x), X(s)) for s in (1, -1)}
    c1 = {s: cp.remote(mb, sb(y, x), Y(s)) for s in (1, -1)}
    a2 = {(0, s): cp.remote(ma, sa(y, x), Y(s)) for s in (1, -1)}
    c2 = {(0, s): cp.remote(mb, sb(y, x), X(s)) for s in (1, -1)}
    gl = cp.here(MS, G.at[:, y, x])
    i64, s64 = iota((64, 64), 0), iota((64, 64), 1)
    order = (s64 == (i64 // 8 % 2) * 32 + (i64 % 8) * 4 + i64 // 16).astype(f32).astype(bf)
    for n in range(4):
        cs = slice(2048 * n, 2048 * (n + 1))
        v = jnp.dot(order, kvw[:, :, cs].reshape(64, 2048), preferred_element_type=f32)
        KVS[:, :, cs] = v.astype(bf).reshape(4, 16, 2048)
    li, ll = iota((128, 128), 0), iota((128, 128), 1)
    rows = []
    flat = jnp.concatenate([kvb[0:1, :], kvb[1:2, :], jnp.zeros((1, 64), f32)], axis=1)
    down = jnp.broadcast_to(flat, (128, 128)).T
    for j in range(4):
        keep = (li == (ll // 8) * 32 + (ll % 8) * 4 + j) & (ll < 16)
        rows.append(jnp.sum(jnp.where(keep, down, 0.0), axis=0, keepdims=True))
    KBS[...] = jnp.concatenate(rows + [jnp.zeros((4, 128), f32)], axis=0)
    own4 = jnp.broadcast_to(jnp.concatenate([owner[...]] * 4, axis=1), (8, 128))
    slot2 = jnp.broadcast_to(jnp.concatenate([slots[...]] * 2, axis=1), (8, 128))
    t0, t1 = iota((8, 128), 0), iota((8, 128), 1)
    INS[...] = jnp.where((t0 == 0) & (t1 // 32 == x), own4,
                         jnp.where((t0 == 1 + x // 2) & (t1 // 64 == x % 2), slot2, 0))
    KVX[x] = KVS[:, :, cols(x)]
    kb[y, x] = KBS[...]
    info[x] = INS[...]

    af, cf = {}, {}
    for s in (1, -1):
        hf = first if s == 1 else second
        a1[s].wait_recv()
        xs = md(x, -s)
        at = G.at[hf, y, xs, :, ca]
        af[s] = cp.remote(at, at, X(s))
        for t in (1, -1):
            a2[(-s, t)] = cp.remote(sa(y, xs), sa(y, xs), Y(t))
        c1[s].wait_recv()
        ys = md(y, -s)
        at = G.at[hf, ys, x, :, cb]
        cf[s] = cp.remote(at, at, Y(s))
        for t in (1, -1):
            c2[(-s, t)] = cp.remote(sb(ys, x), sb(ys, x), X(t))
    last = []

    def pass_on(p):
        for t in (1, -1):
            hf = first if t == 1 else second
            a2[(p, t)].wait_recv()
            at = G.at[hf, md(y, -t), md(x, p), :, ca]
            last.append(cp.remote(at, at, Y(t), "last"))
            c2[(p, t)].wait_recv()
            at = G.at[hf, md(y, p), md(x, -t), :, cb]
            last.append(cp.remote(at, at, X(t), "last"))

    qr = [cp.remote(qw.at[q_half(xo, i), :], RQ.at[i], X(1 - 2 * i)) for i in range(2)]
    qd = [cp.remote(qw.at[cols(md(x, s)), :], wq.at[x, mine, :], X(s), "qd") for s in (1, -1)]
    wx = []
    for t in (1, 3, 2):
        wx.append(cp.remote(KVS.at[:, :, cols(md(x, t))], KVX.at[x], X(t), "wx0"))
        wx.append(cp.remote(KBS, kb.at[y, x], X(t), "wx1"))
        wx.append(cp.remote(INS, info.at[x], X(t), "wx2"))
    for c in w2r:
        c.wait_recv()
    w2f = [cp.remote(RW.at[i], W2.at[md(x, 2 * i - 1), w2_half[i], mine], X(1 - 2 * i)) for i in range(2)]
    w2_mid(0)
    w2d[0].wait_recv()
    w2_start(-1)
    w2d[1].wait_recv()
    w2_start(1)
    pass_on(0)

    def piece(name, r, half=None):
        h = pl.ds(0, 4) if half is None else (first, second)[half]
        if name == "q":
            return wq.at[h, bands(r), :]
        return wkv.at[h, :, :, bands(r)]

    zs, ds_, zf = {}, {}, {}

    def z_start(name):
        zs[name] = {s: cp.remote(piece(name, e), piece(name, e), Z(s)) for s in (1, -1)}
        ds_[name] = [cp.remote(piece(name, e), piece(name, e), other, "d" + name)]

    def z_mid(name):
        zf[name] = {}
        for s in (1, -1):
            zs[name][s].wait_recv()
            r, h = lax.rem(e - 2 * s + 8, 8), 0 if s == 1 else 1
            zf[name][s] = cp.remote(piece(name, r, h), piece(name, r, h), Z(s))
            ds_[name].append(cp.remote(piece(name, r), piece(name, r), other, "d" + name))

    def z_end(name):
        for s in (1, -1):
            zf[name][s].wait_recv()
        r = lax.rem(e + 4, 8)
        ds_[name].append(cp.remote(piece(name, r), piece(name, r), other, "d" + name))

    def z_all(name):
        cp.join("d" + name, wq.at[:, 0:1024, :] if name == "q" else wkv.at[:, :, :, 0:1024])

    for s in (1, -1):
        af[s].wait_recv()
        cf[s].wait_recv()
    xf, yf = md(x, 2), md(y, 2)
    for t in (1, -1):
        a2[(2, t)] = cp.remote(sa(y, xf), sa(y, xf), Y(t))
        c2[(2, t)] = cp.remote(sb(yf, x), sb(yf, x), X(t))
    pass_on(-1)
    pass_on(1)
    for c in qr:
        c.wait_recv()
    qf = [cp.remote(RQ.at[i], wq.at[md(x, 2 * i - 1), pl.ds(pl.multiple_of(256 * e + 128 * i, 128), 128), :],
                    X(1 - 2 * i), "qd") for i in range(2)]
    w2_mid(-1)
    w2_mid(1)
    pass_on(2)
    for c in w2f:
        c.wait_recv()
    w2_start(2)
    cp.join("last", G.at[:, 0])
    gl.wait()
    lv[2].wait()
    wide = jnp.concatenate([b1[...].reshape(1, 320), jnp.zeros((1, 64), f32)], axis=1)
    bcol = jnp.broadcast_to(wide, (128, 384)).T[0:320, :]
    bcol = jnp.concatenate([bcol, bcol], axis=1)
    h1 = {}
    for g in range(2):
        acc = None
        for j in range(4):
            p = lax.dot_general(w1v[:, 1280 * j:1280 * (j + 1)], G[j, 2 * g:2 * g + 2].reshape(256, 1280), NT,
                                preferred_element_type=f32)
            acc = p if acc is None else acc + p
        v = acc + bcol
        v = 0.5 * v * (1.0 + lax.erf(v * (0.5 ** 0.5)))
        H[x, :, 256 * g:256 * (g + 1)] = v.astype(bf)
        hc = pl.ds(256 * g, 256)
        for s in (1, -1):
            h1[(g, s)] = cp.remote(H.at[x, :, hc], H.at[x, :, hc], X(s))
    h2 = []

    def pass_hidden(g):
        for s in (1, -1):
            h1[(g, s)].wait_recv()
            at = H.at[md(x, -s), pl.ds(0, 160) if s == 1 else pl.ds(160, 160), pl.ds(256 * g, 256)]
            h2.append(cp.remote(at, at, X(s), "h2"))

    w2_mid(2)
    cp.join("wx0", KVX.at[0:3])
    cp.join("wx1", kb.at[0, 0:3])
    cp.join("wx2", info.at[0:3])
    ky = []
    for s in (1, 2, 3):
        yd = md(y, s)
        ky.append(cp.remote(KVX.at[:, yd], wkv.at[y, :, :, mine], Y(s), "ky0"))
        ky.append(cp.remote(kb.at[y], kb.at[y], Y(s), "ky1"))
    wkv[y, :, :, mine] = KVX[:, y]
    cp.join("qd", wq.at[0, 0:768, :])
    wl[1].wait()
    z_start("q")
    pass_hidden(0)
    for s in (0, -1, 1, 2):
        w2_end(s)
    pass_hidden(1)
    quarter = lambda v: pl.ds(pl.multiple_of(2048 * v, 2048), 2048)
    th = [pl.ds(0, 32), pl.ds(32, 32)]
    tr = [cp.remote(text.at[th[i], quarter(xo)], TR.at[i], X(1 - 2 * i), "tr") for i in range(2)]
    td = [cp.remote(text.at[:, quarter(md(x, s))], T.at[x], X(s), "td") for s in (1, -1)]
    tl = cp.here(text.at[:, quarter(x)], T.at[x])
    tab = info[0] + info[1] + info[2] + info[3]
    own = tab[0:1, :]
    down = jnp.broadcast_to(own.astype(f32), (128, 128)).T.astype(jnp.int32)
    before = (down == own) & (li < ll) & (li // 32 == ll // 32)
    rank = jnp.sum(before.astype(jnp.int32), axis=0, keepdims=True)
    target = own * 32 + (iota((1, 128), 1) // 32) * 8 + rank
    pick = (iota((256, 128), 0) == target).astype(f32).astype(bf)
    choose = []
    for i in range(2):
        s = jnp.broadcast_to(tab[1 + i:2 + i, :].astype(f32), (128, 128)).T.astype(jnp.int32)
        s = jnp.concatenate([s, s], axis=1)
        lane, row = iota((128, 256), 1), iota((128, 256), 0)
        hit = ((lane // 32) * 8 + lane % 8 == s) & ((lane % 32) // 8 == row // 64 + 2 * i)
        choose.append(hit.astype(f32).astype(bf))
    cp.join("ky0", KVX.at[0:3])
    cp.join("ky1", kb.at[0:3])
    z_start("kv")
    wl[0].wait()
    cp.join("dw", W2.at[:, :, 0:1024])
    cp.join("h2", H.at[0])
    HT[...] = H[...].reshape(1280, 512).T

    lo, hi = pl.ds(0, 64), pl.ds(64, 64)
    yr, yl = md(y, 1), md(y, -1)
    ro, rn, hand, handl = {}, {}, {}, {}

    def mul(c):
        cs = slice(512 * c, 512 * (c + 1))
        v = jnp.dot(HT[...], W2[:, :, cs].reshape(1280, 512), preferred_element_type=f32)
        PC[c] = v.astype(bf).reshape(4, 128, 512)
        ro[c] = [cp.remote(PC.at[c, md(y, 2), lo], RO.at[c, 0], Y(1), ("ro", c)),
                 cp.remote(PC.at[c, md(y, 2), hi], RO.at[c, 1], Y(-1), ("ro", c))]
        rn[c] = [cp.remote(PC.at[c, yr, hi], RN.at[c, 0, hi], Y(1), ("rn", c)),
                 cp.remote(PC.at[c, yl, lo], RN.at[c, 1, lo], Y(-1), ("rn", c))]

    def relay_y(c):
        cp.join(("ro", c), RO.at[c])
        PC[c, yr, 0:64, :] = (PC[c, yr, 0:64, :].astype(f32) + RO[c, 0].astype(f32)).astype(bf)
        rn[c].append(cp.remote(PC.at[c, yr, lo], RN.at[c, 0, lo], Y(1), ("rn", c)))
        PC[c, yl, 64:128, :] = (PC[c, yl, 64:128, :].astype(f32) + RO[c, 1].astype(f32)).astype(bf)
        rn[c].append(cp.remote(PC.at[c, yl, hi], RN.at[c, 1, hi], Y(-1), ("rn", c)))

    def give(c):
        cp.join(("rn", c), RN.at[c])
        v = PC[c, y].astype(f32) + RN[c, 0].astype(f32) + RN[c, 1].astype(f32)
        v = (v + b2[:, pl.ds(pl.multiple_of(2048 * x + 512 * c, 512), 512)]).astype(bf)
        SB[c, :, :, 0:512] = jnp.dot(pick, v, preferred_element_type=f32).astype(bf).reshape(8, 32, 512)
        w = pl.ds(0, 512)
        if c == 0:
            v = jnp.dot(pick, jnp.ones((128, 128), bf), preferred_element_type=f32)
            SB[c, :, :, 512:640] = v.astype(bf).reshape(8, 32, 128)
            w = pl.ds(0, 640)
        hand[c] = [cp.remote(SB.at[c, d[0], :, w], R.at[c, dp, :, w], d, ("hand", c)) for d in group]
        handl[c] = cp.here(SB.at[c, dp, :, w], R.at[c, dp, :, w])

    h = [pl.ds(0, 128), pl.ds(128, 128)]
    gx = gain[:, quarter(x)]
    filled, sq, yc = [None, None], [None, None], {1: [], -1: []}

    def take(c):
        cs = slice(512 * c, 512 * (c + 1))
        cp.join(("hand", c), R.at[c, 0:7, :, pl.ds(0, 640 if c == 0 else 512)])
        handl[c].wait()
        for i in range(2):
            if c == 0:
                seen = jnp.dot(choose[i], R[0, :, :, 512:640].reshape(256, 128), preferred_element_type=f32)
                filled[i] = seen[:, 0:1] > 0.5
            v = jnp.dot(choose[i], R[c, :, :, 0:512].reshape(256, 512), preferred_element_type=f32)
            v = jnp.where(filled[i], v, T[2 * i:2 * i + 2, :, cs].reshape(128, 512).astype(f32))
            t = jnp.sum(v * v, axis=1, keepdims=True)
            sq[i] = t if c == 0 else sq[i] + t
            A[y, 128 * i:128 * (i + 1), cs] = (v * gx[:, cs]).astype(bf)
            w, s = pl.ds(512 * c, 512), 1 - 2 * i
            yc[s].append(cp.remote(A.at[y, h[i], w], A.at[y, h[i], w], Y(s), ("yc", s)))

    mul(0)
    mul(1)
    mul(2)
    relay_y(0)
    mul(3)
    relay_y(1)
    z_mid("q")
    give(0)
    cp.join("tr", TR)
    tf = [cp.remote(TR.at[i], T.at[md(x, 2 * i - 1), th[i]], X(1 - 2 * i), "td") for i in range(2)]
    relay_y(2)
    give(1)
    relay_y(3)
    z_mid("kv")
    give(2)
    cp.join("td", T.at[0:3])
    tl.wait()
    give(3)
    z_end("q")
    z_end("kv")
    take(0)
    take(1)
    take(2)
    take(3)
    SS[x] = jnp.concatenate([jnp.broadcast_to(t, (128, 128)).T[0:8, :] for t in sq], axis=1)
    sx = [cp.remote(SS.at[x], SS.at[x], X(s), "sx") for s in (1, 2, 3)]
    z_all("q")
    z_all("kv")

    tag = [0]

    def pair(ga, oa, gb, ob, size):
        tag[0] += 1
        a = jnp.concatenate([A[ga, oa:oa + size, :], A[gb, ob:ob + size, :]], axis=0)
        us = []
        for g, o in ((ga, oa), (gb, ob)):
            at = lambda off, n, g=g, o=o: pl.ds(pl.multiple_of(256 * g + o + off, n), n)
            us.append(dict(tag=tag[0], size=size, rows=at(0, size), lo=at(0, size // 2), hi=at(size // 2, size // 2),
                           share=lambda v, g=g, o=o: pl.ds(
                               pl.multiple_of(256 * g + o + size // 4 * v, size // 4), size // 4),
                           slot=pl.ds(pl.multiple_of(64 * g + o // 4, size // 4), size // 4)))
        prod = lambda s: jnp.dot(a, wq[md(x, s)], preferred_element_type=f32)

        def put(ref, v):
            v = v.astype(ref.dtype)
            for n, u in enumerate(us):
                ref[u["rows"], :] = v[size * n:size * (n + 1)]

        put(QO, prod(2))
        for u in us:
            u["o"] = [cp.remote(QO.at[u["lo"]], RQO.at[0, u["lo"]], X(1), ("o", u["tag"])),
                      cp.remote(QO.at[u["hi"]], RQO.at[1, u["hi"]], X(-1), ("o", u["tag"]))]
        put(KP, lax.dot_general(a, wkv[...].reshape(256, 2048), NT, preferred_element_type=f32))
        for u in us:
            u["k"] = []
            for s in (2, 1, 3):
                u["k"].append(cp.remote(KP.at[u["share"](md(x, s))], RKV.at[x, u["slot"]], X(s), ("k", u["tag"])))
        put(QR, prod(1))
        for u in us:
            u["n"] = [cp.remote(QR.at[u["hi"]], RQN.at[0, u["hi"]], X(1), ("n", u["tag"]))]
        put(QL, prod(-1))
        for u in us:
            u["n"].append(cp.remote(QL.at[u["lo"]], RQN.at[1, u["lo"]], X(-1), ("n", u["tag"])))
        put(Q0, prod(0))
        return us

    def relay(us):
        cp.join(("o", us[0]["tag"]), RQO.at[0, 0:2 * us[0]["size"]])
        for u in us:
            lo, hi = u["lo"], u["hi"]
            QR[lo, :] = (QR[lo, :].astype(f32) + RQO[0, lo, :].astype(f32)).astype(bf)
            u["n"].append(cp.remote(QR.at[lo], RQN.at[0, lo], X(1), ("n", u["tag"])))
            QL[hi, :] = (QL[hi, :].astype(f32) + RQO[1, hi, :].astype(f32)).astype(bf)
            u["n"].append(cp.remote(QL.at[hi], RQN.at[1, hi], X(-1), ("n", u["tag"])))

    bias = jnp.concatenate([kb[p // 4, p % 4, pl.ds(y, 1), 0:16] for p in range(16)], axis=1)

    def keys(us):
        cp.join(("k", us[0]["tag"]), KP.at[0:3 * us[0]["size"] // 2])
        for u in us:
            m = u["share"](x)
            v = KP[m, :].astype(f32)
            for s in (1, 2, 3):
                v = v + RKV[md(x, s), u["slot"]].astype(f32)
            sc = SC[m, :]
            v = v * jnp.concatenate([sc, sc], axis=1) + bias
            kv_out[m, :] = v.astype(bf)
            u["f"] = [cp.remote(kv_out.at[m], kv_out.at[m], X(s), ("f", u["tag"])) for s in (2, 1, 3)]

    def scale(g):
        v = lax.rsqrt(SY[g] * (1.0 / 8192.0) + 1e-6)
        for i in range(2):
            SC[pl.ds(pl.multiple_of(256 * g + 128 * i, 128), 128), :] = jnp.broadcast_to(
                v[0:1, 128 * i:128 * (i + 1)], (128, 128)).T

    def finish(us):
        cp.join(("n", us[0]["tag"]), RQN.at[0, 0:4 * us[0]["size"]])
        for u in us:
            rows = u["rows"]
            sc = SC[rows, :]
            v = Q0[rows, :] + RQN[0, rows, :].astype(f32) + RQN[1, rows, :].astype(f32)
            q_out[rows, :] = (v * jnp.concatenate([sc, sc], axis=1) + qb[...]).astype(bf)
        cp.join(("f", us[0]["tag"]), KP.at[0:3 * us[0]["size"] // 2])

    u0 = pair(y, 0, y, 128, 128)
    cp.join("sx", SS.at[0:3])
    SY[y] = SS[0] + SS[1] + SS[2] + SS[3]
    sy = [cp.remote(SY.at[y], SY.at[y], Y(s), "sy") for s in (1, 2, 3)]
    band = lambda o: pl.ds(o, 64)
    yo = {1: [cp.remote(A.at[y, band(o)], A.at[y, band(o)], Y(1)) for o in (128, 192)],
          -1: [cp.remote(A.at[y, band(o)], A.at[y, band(o)], Y(-1)) for o in (0, 64)]}
    scale(y)
    relay(u0)
    up, dn, op = yr, yl, md(y, 2)
    far = {}
    cp.join(("yc", 1), A.at[0, h[0]])
    far[1] = [cp.remote(A.at[dn, band(o)], A.at[dn, band(o)], Y(1)) for o in (0, 64)]
    cp.join(("yc", -1), A.at[0, h[0]])
    far[-1] = [cp.remote(A.at[up, band(o)], A.at[up, band(o)], Y(-1)) for o in (128, 192)]
    keys(u0)
    u1 = pair(dn, 0, up, 128, 128)
    finish(u0)
    relay(u1)
    yo[1][0].wait_recv()
    yo[-1][0].wait_recv()
    cp.join("sy", SY.at[0:3])
    for g in (dn, up, op):
        scale(g)
    u2 = pair(dn, 128, up, 0, 64)
    keys(u1)
    relay(u2)
    yo[1][1].wait_recv()
    yo[-1][1].wait_recv()
    u3 = pair(dn, 192, up, 64, 64)
    keys(u2)
    finish(u1)
    relay(u3)
    far[1][0].wait_recv()
    far[-1][0].wait_recv()
    u4 = pair(op, 0, op, 128, 64)
    keys(u3)
    finish(u2)
    relay(u4)
    far[1][1].wait_recv()
    far[-1][1].wait_recv()
    u5 = pair(op, 64, op, 192, 64)
    keys(u4)
    finish(u3)
    relay(u5)
    keys(u5)
    finish(u4)
    finish(u5)
    cp.drain()
    assert len(cp.groups) == N3, len(cp.groups)


def whole(patches, ids, owner, slots, text, vnorm, qkv_w, qkv_b, out_w, mnorm, w1, b1, w2, b2, gain, qw, qb, kvw, kvb):
    bf, f32, i32 = jnp.bfloat16, jnp.float32, jnp.int32
    V, ANY = pl.BlockSpec(memory_space=pltpu.VMEM), pl.BlockSpec(memory_space=pl.ANY)
    S = jax.ShapeDtypeStruct
    M = pltpu.VMEM
    return pl.pallas_call(
        whole_kernel,
        out_shape=(S((1024, 256), bf), S((1024, 256), bf)),
        in_specs=[V, V, V, V, ANY, V, ANY, V, ANY, V, ANY, V, ANY, V, V, ANY, V, V, V],
        out_specs=[V] * 2,
        scratch_shapes=[
            M((4, 32, 1280), bf),
            M((4, 4, 4, 32, 1280), bf),
            M((1280, 1920), bf),
            M((640, 1280), bf),
            M((320, 5120), bf),
            M((4, 320, 512), bf),
            M((512, 1280), bf),
            M((4, 320, 2048), bf),
            M((4, 2048, 256), bf),
            M((4, 4, 16, 2048), bf),
            M((4, 16, 8192), bf),
            M((4, 4, 16, 256), bf),
            M((8, 128), f32),
            M((4, 4, 8, 128), f32),
            M((8, 128), i32),
            M((4, 8, 128), i32),
            M((2, 160, 256), bf),
            M((2, 128, 256), bf),
            M((4, 4, 128, 512), bf),
            M((4, 2, 64, 512), bf),
            M((4, 2, 128, 512), bf),
            M((4, 64, 2048), bf),
            M((2, 32, 2048), bf),
            M((4, 8, 32, 640), bf),
            M((4, 8, 32, 640), bf),
            M((4, 256, 2048), bf),
            M((4, 8, 256), f32),
            M((4, 8, 256), f32),
            M((1024, 128), f32),
            M((1024, 256), f32),
            M((1024, 256), bf),
            M((1024, 256), bf),
            M((1024, 256), bf),
            M((2, 1024, 256), bf),
            M((2, 1024, 256), bf),
            M((1024, 256), bf),
            M((4, 256, 256), bf),
            pltpu.SemaphoreType.DMA((N3,)),
            pltpu.SemaphoreType.DMA((N3,)),
            pltpu.SemaphoreType.DMA((16,)),
        ],
        compiler_params=pltpu.CompilerParams(collective_id=1, has_side_effects=True, vmem_limit_bytes=64000000),
        name="whole",
    )(patches, ids, owner, slots, text, vnorm, qkv_w, qkv_b, out_w, mnorm, w1, b1, w2, b2, gain, qw, qb, kvw, kvb)


def attention_kernel(q, kv, out):
    bf, f32 = jnp.bfloat16, jnp.float32
    c, d = lax.broadcasted_iota(jnp.int32, (256, 128), 0), lax.broadcasted_iota(jnp.int32, (256, 128), 1)
    spot = (d // 8) * 16 + d % 8
    keys = jnp.dot(kv[...], (c == spot).astype(f32).astype(bf), preferred_element_type=f32).astype(bf)
    values = jnp.dot(kv[...], (c == spot + 8).astype(f32).astype(bf), preferred_element_type=f32).astype(bf)
    low = lax.broadcasted_iota(jnp.int32, (256, 256), 0) >= lax.broadcasted_iota(jnp.int32, (256, 256), 1)
    k = HD ** (-0.5) * 1.4426950408889634
    for i in range(4):
        rows = slice(256 * i, 256 * (i + 1))
        for h in range(2):
            hs = slice(128 * h, 128 * (h + 1))
            s = lax.dot_general(q[rows, hs], keys[rows], NT, preferred_element_type=f32)
            s = jnp.where(low, s, -1e30)
            top = jnp.max(s, axis=1, keepdims=True)
            if i:
                before = lax.dot_general(q[rows, hs], keys[:256 * i], NT, preferred_element_type=f32)
                top = jnp.maximum(top, jnp.max(before, axis=1, keepdims=True))
            p = jnp.exp2((s - top) * k)
            total = jnp.sum(p, axis=1, keepdims=True)
            m = jnp.dot(p.astype(bf), values[rows], preferred_element_type=f32)
            if i:
                p = jnp.exp2((before - top) * k)
                total = total + jnp.sum(p, axis=1, keepdims=True)
                m = m + jnp.dot(p.astype(bf), values[:256 * i], preferred_element_type=f32)
            out[rows, hs] = (m / total).astype(bf)


def attention(q, kv):
    V = pl.BlockSpec(memory_space=pltpu.VMEM)
    return pl.pallas_call(
        attention_kernel,
        out_shape=jax.ShapeDtypeStruct((1024, 256), jnp.bfloat16),
        in_specs=[V, V],
        out_specs=V,
        compiler_params=pltpu.CompilerParams(vmem_limit_bytes=60000000),
        name="attention",
    )(q, kv)


def shards(
    patches,
    window_ids,
    owner,
    slot_of_row,
    text_embeds,
    vit_norm,
    vit_qkv_w,
    vit_qkv_b,
    vit_out_w,
    merge_norm,
    merge_w1,
    merge_b1,
    merge_w2,
    merge_b2,
    llm_norm,
    q_w,
    q_b,
    kv_w,
    kv_b,
):
    q, kv = whole(
        patches, window_ids, owner.reshape(1, 32), slot_of_row, text_embeds, vit_norm, vit_qkv_w,
        vit_qkv_b, vit_out_w, merge_norm, merge_w1.T, merge_b1, merge_w2, merge_b2[None],
        llm_norm[None], q_w, q_b[None], kv_w.transpose(0, 2, 1), kv_b,
    )
    return attention(q, kv)


def solution(mesh):
    return jax.shard_map(
        shards,
        mesh=mesh,
        in_specs=(
            P(("dp", "mp"), None),
            P(("dp", "mp"), None),
            P(("dp", "mp"), None),
            P(("dp", "mp"), None),
            P(("dp", "mp"), None),
            P(),
            P(),
            P(),
            P(),
            P(),
            P(None, "mp"),
            P("mp"),
            P("mp", None),
            P(),
            P(),
            P(None, "mp"),
            P("mp"),
            P(None, None, "mp"),
            P(None, "mp"),
        ),
        out_specs=P("dp", "mp"),
        check_vma=False,
    )
```

time: 157 us -> 140 us (0.89)
  Pallas kernels: 152 us -> 140 us
  local copies, waits for them, and re-layouts: 5.13 us -> 0 us
    pallas_call x1, Pallas kernels: 146 us -> 135 us  [whole(): pl.pallas_call(whole_kernel, out_shape=(S((1024, 256), bf), S((1024, 256)...]
    broadcast_in_dim x4 -> x0, local copies, waits for them, and re-layouts: 5.13 us -> none  [the longest x1 1.3 us: shards(): vit_qkv_b[None]]
where the time goes in v4:
time: 140 us
  Pallas kernels  140 us (100%)
    pallas_call x1, Pallas kernels, whole(): pl.pallas_call(whole_kernel, out_shape=(S((1024, 256), bf), S((1024, 256)...  135 us
    pallas_call x1, Pallas kernels, attention(): pl.pallas_call(attention_kernel, out_shape=jax.ShapeDtypeStruct((1024, 25...  5.21 us

profile of v4, /device:TPU:0, one launch (start us, length us, event | category | flops | bytes accessed | tf_op | source)
XLA Modules:
  0.0 139.8 jit_solution(1878795449907122717)
XLA Ops:
  0.0 134.6 %whole.1 = (bf16[1024,256]{1,0:T(8,128)(2,1)}, bf16[1024,256]{1,0:T(8,128)(2,1)}) custom-call(bf16[128,1280]{1,0:T(8,128)(2,1)} %patches.1, s32[1,128]{1,0:T(1,128)} %ids.1, s32[1,32]{1,0:T(1,128)} %bitcast.11, s32[1,64]{1,0:T(1,128)} %slots.1, bf16[64,8192]{1,0:T(8,128)(2,1)} %text.1, f32[1280]{0:T(1024)} %vnorm.1, bf16[1280,1920]{1,0:T(8,128)(2,1)} %qkv_w.1, ...), custom_call_target="tpu_custom_call" | custom-call | tf_op jit(solution)/shard_map/whole/pallas_call | solution.py:566
  134.6 5.2 %attention.1 = bf16[1024,256]{1,0:T(8,128)(2,1)} custom-call(bf16[1024,256]{1,0:T(8,128)(2,1)} %get-tuple-element.7.q, bf16[1024,256]{1,0:T(8,128)(2,1)} %get-tuple-element.8.kv), custom_call_target="tpu_custom_call" | custom-call | tf_op jit(solution)/shard_map/attention/pallas_call | solution.py:648

commit v5 on v4

--- a/solution.py
+++ b/solution.py
@@ -404,27 +404,27 @@
 
     mul(0)
     mul(1)
+    relay_y(0)
     mul(2)
-    relay_y(0)
+    relay_y(1)
     mul(3)
-    relay_y(1)
     z_mid("q")
     give(0)
     cp.join("tr", TR)
     tf = [cp.remote(TR.at[i], T.at[md(x, 2 * i - 1), th[i]], X(1 - 2 * i), "td") for i in range(2)]
     relay_y(2)
+    z_mid("kv")
     give(1)
     relay_y(3)
-    z_mid("kv")
     give(2)
     cp.join("td", T.at[0:3])
     tl.wait()
     give(3)
-    z_end("q")
-    z_end("kv")
     take(0)
     take(1)
+    z_end("q")
     take(2)
+    z_end("kv")
     take(3)
     SS[x] = jnp.concatenate([jnp.broadcast_to(t, (128, 128)).T[0:8, :] for t in sq], axis=1)
     sx = [cp.remote(SS.at[x], SS.at[x], X(s), "sx") for s in (1, 2, 3)]
@@ -544,10 +544,10 @@
     u4 = pair(op, 0, op, 128, 64)
     keys(u3)
     finish(u2)
-    relay(u4)
     far[1][1].wait_recv()
     far[-1][1].wait_recv()
     u5 = pair(op, 64, op, 192, 64)
+    relay(u4)
     keys(u4)
     finish(u3)
     relay(u5)

time: 140 us -> 138 us (0.986)
  Pallas kernels: 140 us -> 138 us
    pallas_call x1, Pallas kernels: 135 us -> 133 us  [whole(): pl.pallas_call(whole_kernel, out_shape=(S((1024, 256), bf), S((1024, 256)...]
where the time goes in v5:
time: 138 us
  Pallas kernels  138 us (100%)
    pallas_call x1, Pallas kernels, whole(): pl.pallas_call(whole_kernel, out_shape=(S((1024, 256), bf), S((1024, 256)...  133 us
    pallas_call x1, Pallas kernels, attention(): pl.pallas_call(attention_kernel, out_shape=jax.ShapeDtypeStruct((1024, 25...  5.21 us

profile of v5, /device:TPU:0, one launch (start us, length us, event | category | flops | bytes accessed | tf_op | source)
XLA Modules:
  0.0 137.9 jit_solution(8982128152299317886)
XLA Ops:
  0.0 132.6 %whole.1 = (bf16[1024,256]{1,0:T(8,128)(2,1)}, bf16[1024,256]{1,0:T(8,128)(2,1)}) custom-call(bf16[128,1280]{1,0:T(8,128)(2,1)} %patches.1, s32[1,128]{1,0:T(1,128)} %ids.1, s32[1,32]{1,0:T(1,128)} %bitcast.11, s32[1,64]{1,0:T(1,128)} %slots.1, bf16[64,8192]{1,0:T(8,128)(2,1)} %text.1, f32[1280]{0:T(1024)} %vnorm.1, bf16[1280,1920]{1,0:T(8,128)(2,1)} %qkv_w.1, ...), custom_call_target="tpu_custom_call" | custom-call | tf_op jit(solution)/shard_map/whole/pallas_call | solution.py:566
  132.6 5.2 %attention.1 = bf16[1024,256]{1,0:T(8,128)(2,1)} custom-call(bf16[1024,256]{1,0:T(8,128)(2,1)} %get-tuple-element.7.q, bf16[1024,256]{1,0:T(8,128)(2,1)} %get-tuple-element.8.kv), custom_call_target="tpu_custom_call" | custom-call | tf_op jit(solution)/shard_map/attention/pallas_call | solution.py:648

commit v6 on v5

--- a/solution.py
+++ b/solution.py
@@ -14,26 +14,25 @@
 class Copies:
     def __init__(self, send, recv, local):
         self.send, self.recv, self.local = send, recv, local
-        self.groups, self.views, self.m, self.n = {}, {}, 0, 0
-        self.sent = []
-
-    def remote(self, src, dst, dev, group=None):
-        single = group is None
-        if single:
+        self.groups, self.outs, self.views, self.m, self.n = {}, {}, {}, 0, 0
+
+    def remote(self, src, dst, dev, group=None, out=None):
+        if group is None:
             self.n += 1
             group = self.n
+        if out is None:
+            out = group[0] if isinstance(group, tuple) and group[0] in "o n k f ro rn".split() else group
+        j = self.outs.setdefault(out, len(self.outs))
         k = self.groups.setdefault(group, len(self.groups))
         c = pltpu.make_async_remote_copy(
-            src_ref=src, dst_ref=dst, send_sem=self.send.at[k], recv_sem=self.recv.at[k],
+            src_ref=src, dst_ref=dst, send_sem=self.send.at[j], recv_sem=self.recv.at[k],
             device_id=dev, device_id_type=MESH)
         c.start()
-        if single:
-            self.sent.append(c)
         return c
 
     def join(self, group, view):
         k = self.groups[group]
-        self.views[k] = view
+        self.views[group] = view
         pltpu.make_async_copy(view, view, self.recv.at[k]).wait()
 
     def here(self, src, dst):
@@ -43,12 +42,10 @@
         c.start()
         return c
 
-    def drain(self):
-        for c in self.sent:
-            c.wait_send()
-        for k, view in self.views.items():
-            pltpu.make_async_copy(view, view, self.send.at[k]).wait()
-        assert len(self.sent) + len(self.views) == len(self.groups)
+    def drain(self, views):
+        for out, j in self.outs.items():
+            view = views[out] if out in views else self.views[out]
+            pltpu.make_async_copy(view, view, self.send.at[j]).wait()
 
 
 def places():
@@ -69,6 +66,7 @@
 
 
 N3 = 117
+N4 = 32
 
 
 def vision(patches, ids, norm, qkv_w, qkv_b, out_w, gain):
@@ -131,7 +129,7 @@
     def w2_start(s):
         xs = md(x, s)
         src = w2.at[:, cols(x)] if s == 0 else W2.at[xs, :, mine]
-        zw[s] = {t: cp.remote(src, W2.at[xs, :, mine], Z(t)) for t in (1, -1)}
+        zw[s] = {t: cp.remote(src, W2.at[xs, :, mine], Z(t), out="w") for t in (1, -1)}
         dw.append(cp.remote(src, W2.at[xs, :, mine], other, "dw"))
 
     def w2_mid(s):
@@ -140,7 +138,7 @@
             zw[s][t].wait_recv()
             at = W2.at[xs, :, bands(lax.rem(e - 2 * t + 8, 8))]
             if t == way:
-                zwf[s] = cp.remote(at, at, Z(t))
+                zwf[s] = cp.remote(at, at, Z(t), out="w")
             dw.append(cp.remote(at, at, other, "dw"))
 
     def w2_end(s):
@@ -148,8 +146,8 @@
         at = W2.at[md(x, s), :, bands(lax.rem(e + 4, 8))]
         dw.append(cp.remote(at, at, other, "dw"))
 
-    w2r = [cp.remote(w2.at[w2_half[i], cols(xo)], RW.at[i], X(1 - 2 * i)) for i in range(2)]
-    w2d = [cp.remote(w2.at[:, cols(md(x, s))], W2.at[x, :, mine], X(s)) for s in (1, -1)]
+    w2r = [cp.remote(w2.at[w2_half[i], cols(xo)], RW.at[i], X(1 - 2 * i), out="w") for i in range(2)]
+    w2d = [cp.remote(w2.at[:, cols(md(x, s))], W2.at[x, :, mine], X(s), out="w") for s in (1, -1)]
     w2_start(0)
     wl = [cp.here(w2.at[:, cols(x)], W2.at[x, :, mine]), cp.here(qw.at[cols(x), :], wq.at[x, mine, :])]
 
@@ -158,10 +156,10 @@
     MS[...] = vision(patches, ids, vnorm, QKVW, qkv_b, OUTW, mnorm).reshape(4, 32, 1280)
 
     ma, mb = MS.at[:, :, ca], MS.at[:, :, cb]
-    a1 = {s: cp.remote(ma, sa(y, x), X(s)) for s in (1, -1)}
-    c1 = {s: cp.remote(mb, sb(y, x), Y(s)) for s in (1, -1)}
-    a2 = {(0, s): cp.remote(ma, sa(y, x), Y(s)) for s in (1, -1)}
-    c2 = {(0, s): cp.remote(mb, sb(y, x), X(s)) for s in (1, -1)}
+    a1 = {s: cp.remote(ma, sa(y, x), X(s), out="g") for s in (1, -1)}
+    c1 = {s: cp.remote(mb, sb(y, x), Y(s), out="g") for s in (1, -1)}
+    a2 = {(0, s): cp.remote(ma, sa(y, x), Y(s), out="g") for s in (1, -1)}
+    c2 = {(0, s): cp.remote(mb, sb(y, x), X(s), out="g") for s in (1, -1)}
     gl = cp.here(MS, G.at[:, y, x])
     i64, s64 = iota((64, 64), 0), iota((64, 64), 1)
     order = (s64 == (i64 // 8 % 2) * 32 + (i64 % 8) * 4 + i64 // 16).astype(f32).astype(bf)
@@ -192,15 +190,15 @@
         a1[s].wait_recv()
         xs = md(x, -s)
         at = G.at[hf, y, xs, :, ca]
-        af[s] = cp.remote(at, at, X(s))
+        af[s] = cp.remote(at, at, X(s), out="g")
         for t in (1, -1):
-            a2[(-s, t)] = cp.remote(sa(y, xs), sa(y, xs), Y(t))
+            a2[(-s, t)] = cp.remote(sa(y, xs), sa(y, xs), Y(t), out="g")
         c1[s].wait_recv()
         ys = md(y, -s)
         at = G.at[hf, ys, x, :, cb]
-        cf[s] = cp.remote(at, at, Y(s))
+        cf[s] = cp.remote(at, at, Y(s), out="g")
         for t in (1, -1):
-            c2[(-s, t)] = cp.remote(sb(ys, x), sb(ys, x), X(t))
+            c2[(-s, t)] = cp.remote(sb(ys, x), sb(ys, x), X(t), out="g")
     last = []
 
     def pass_on(p):
@@ -213,7 +211,7 @@
             at = G.at[hf, md(y, p), md(x, -t), :, cb]
             last.append(cp.remote(at, at, X(t), "last"))
 
-    qr = [cp.remote(qw.at[q_half(xo, i), :], RQ.at[i], X(1 - 2 * i)) for i in range(2)]
+    qr = [cp.remote(qw.at[q_half(xo, i), :], RQ.at[i], X(1 - 2 * i), out="z") for i in range(2)]
     qd = [cp.remote(qw.at[cols(md(x, s)), :], wq.at[x, mine, :], X(s), "qd") for s in (1, -1)]
     wx = []
     for t in (1, 3, 2):
@@ -222,7 +220,7 @@
         wx.append(cp.remote(INS, info.at[x], X(t), "wx2"))
     for c in w2r:
         c.wait_recv()
-    w2f = [cp.remote(RW.at[i], W2.at[md(x, 2 * i - 1), w2_half[i], mine], X(1 - 2 * i)) for i in range(2)]
+    w2f = [cp.remote(RW.at[i], W2.at[md(x, 2 * i - 1), w2_half[i], mine], X(1 - 2 * i), out="w") for i in range(2)]
     w2_mid(0)
     w2d[0].wait_recv()
     w2_start(-1)
@@ -239,7 +237,7 @@
     zs, ds_, zf = {}, {}, {}
 
     def z_start(name):
-        zs[name] = {s: cp.remote(piece(name, e), piece(name, e), Z(s)) for s in (1, -1)}
+        zs[name] = {s: cp.remote(piece(name, e), piece(name, e), Z(s), out="z") for s in (1, -1)}
         ds_[name] = [cp.remote(piece(name, e), piece(name, e), other, "d" + name)]
 
     def z_mid(name):
@@ -247,7 +245,7 @@
         for s in (1, -1):
             zs[name][s].wait_recv()
             r, h = lax.rem(e - 2 * s + 8, 8), 0 if s == 1 else 1
-            zf[name][s] = cp.remote(piece(name, r, h), piece(name, r, h), Z(s))
+            zf[name][s] = cp.remote(piece(name, r, h), piece(name, r, h), Z(s), out="z")
             ds_[name].append(cp.remote(piece(name, r), piece(name, r), other, "d" + name))
 
     def z_end(name):
@@ -264,8 +262,8 @@
         cf[s].wait_recv()
     xf, yf = md(x, 2), md(y, 2)
     for t in (1, -1):
-        a2[(2, t)] = cp.remote(sa(y, xf), sa(y, xf), Y(t))
-        c2[(2, t)] = cp.remote(sb(yf, x), sb(yf, x), X(t))
+        a2[(2, t)] = cp.remote(sa(y, xf), sa(y, xf), Y(t), out="g")
+        c2[(2, t)] = cp.remote(sb(yf, x), sb(yf, x), X(t), out="g")
     pass_on(-1)
     pass_on(1)
     for c in qr:
@@ -296,7 +294,7 @@
         H[x, :, 256 * g:256 * (g + 1)] = v.astype(bf)
         hc = pl.ds(256 * g, 256)
         for s in (1, -1):
-            h1[(g, s)] = cp.remote(H.at[x, :, hc], H.at[x, :, hc], X(s))
+            h1[(g, s)] = cp.remote(H.at[x, :, hc], H.at[x, :, hc], X(s), out="h")
     h2 = []
 
     def pass_hidden(g):
@@ -511,16 +509,16 @@
     SY[y] = SS[0] + SS[1] + SS[2] + SS[3]
     sy = [cp.remote(SY.at[y], SY.at[y], Y(s), "sy") for s in (1, 2, 3)]
     band = lambda o: pl.ds(o, 64)
-    yo = {1: [cp.remote(A.at[y, band(o)], A.at[y, band(o)], Y(1)) for o in (128, 192)],
-          -1: [cp.remote(A.at[y, band(o)], A.at[y, band(o)], Y(-1)) for o in (0, 64)]}
+    yo = {1: [cp.remote(A.at[y, band(o)], A.at[y, band(o)], Y(1), out="a") for o in (128, 192)],
+          -1: [cp.remote(A.at[y, band(o)], A.at[y, band(o)], Y(-1), out="a") for o in (0, 64)]}
     scale(y)
     relay(u0)
     up, dn, op = yr, yl, md(y, 2)
     far = {}
     cp.join(("yc", 1), A.at[0, h[0]])
-    far[1] = [cp.remote(A.at[dn, band(o)], A.at[dn, band(o)], Y(1)) for o in (0, 64)]
+    far[1] = [cp.remote(A.at[dn, band(o)], A.at[dn, band(o)], Y(1), out="a") for o in (0, 64)]
     cp.join(("yc", -1), A.at[0, h[0]])
-    far[-1] = [cp.remote(A.at[up, band(o)], A.at[up, band(o)], Y(-1)) for o in (128, 192)]
+    far[-1] = [cp.remote(A.at[up, band(o)], A.at[up, band(o)], Y(-1), out="a") for o in (128, 192)]
     keys(u0)
     u1 = pair(dn, 0, up, 128, 128)
     finish(u0)
@@ -554,8 +552,9 @@
     keys(u5)
     finish(u4)
     finish(u5)
-    cp.drain()
-    assert len(cp.groups) == N3, len(cp.groups)
+    cp.drain({"w": W2.at[:, :, 0:1024], "g": W2.at[:, :, 0:1408], "z": wq.at[:, 0:1024, :], "h": H.at[0:2],
+              "a": A.at[0:2], "o": RQO.at[0], "n": RQN, "k": KP.at[0:768], "f": KP.at[0:768], "ro": RO, "rn": RN})
+    assert len(cp.groups) == N3 and len(cp.outs) == N4, len(cp.outs)
 
 
 def whole(patches, ids, owner, slots, text, vnorm, qkv_w, qkv_b, out_w, mnorm, w1, b1, w2, b2, gain, qw, qb, kvw, kvb):
@@ -606,7 +605,7 @@
             M((2, 1024, 256), bf),
             M((1024, 256), bf),
             M((4, 256, 256), bf),
-            pltpu.SemaphoreType.DMA((N3,)),
+            pltpu.SemaphoreType.DMA((N4,)),
             pltpu.SemaphoreType.DMA((N3,)),
             pltpu.SemaphoreType.DMA((16,)),
         ],

time: 138 us -> 137 us (level)
  no operation moved by 1% of the time
where the time goes in v6:
time: 137 us
  Pallas kernels  137 us (100%)
    pallas_call x1, Pallas kernels, whole(): pl.pallas_call(whole_kernel, out_shape=(S((1024, 256), bf), S((1024, 256)...  132 us
    pallas_call x1, Pallas kernels, attention(): pl.pallas_call(attention_kernel, out_shape=jax.ShapeDtypeStruct((1024, 25...  5.2 us

profile of v6, /device:TPU:0, one launch (start us, length us, event | category | flops | bytes accessed | tf_op | source)
XLA Modules:
  0.0 137.0 jit_solution(1647024799633234743)
XLA Ops:
  0.0 131.7 %whole.1 = (bf16[1024,256]{1,0:T(8,128)(2,1)}, bf16[1024,256]{1,0:T(8,128)(2,1)}) custom-call(bf16[128,1280]{1,0:T(8,128)(2,1)} %patches.1, s32[1,128]{1,0:T(1,128)} %ids.1, s32[1,32]{1,0:T(1,128)} %bitcast.11, s32[1,64]{1,0:T(1,128)} %slots.1, bf16[64,8192]{1,0:T(8,128)(2,1)} %text.1, f32[1280]{0:T(1024)} %vnorm.1, bf16[1280,1920]{1,0:T(8,128)(2,1)} %qkv_w.1, ...), custom_call_target="tpu_custom_call" | custom-call | tf_op jit(solution)/shard_map/whole/pallas_call | solution.py:565
  131.7 5.2 %attention.1 = bf16[1024,256]{1,0:T(8,128)(2,1)} custom-call(bf16[1024,256]{1,0:T(8,128)(2,1)} %get-tuple-element.7.q, bf16[1024,256]{1,0:T(8,128)(2,1)} %get-tuple-element.8.kv), custom_call_target="tpu_custom_call" | custom-call | tf_op jit(solution)/shard_map/attention/pallas_call | solution.py:647

commit v7 on v6

--- a/solution.py
+++ b/solution.py
@@ -21,7 +21,7 @@
             self.n += 1
             group = self.n
         if out is None:
-            out = group[0] if isinstance(group, tuple) and group[0] in "o n k f ro rn".split() else group
+            out = group[0] if isinstance(group, tuple) and group[0] in ("o", "n", "k", "f", "ro", "rn") else group
         j = self.outs.setdefault(out, len(self.outs))
         k = self.groups.setdefault(group, len(self.groups))
         c = pltpu.make_async_remote_copy(

time: 137 us -> 137 us (level)
  no operation moved by 1% of the time
where the time goes in v7:
time: 137 us
  Pallas kernels  137 us (100%)
    pallas_call x1, Pallas kernels, whole(): pl.pallas_call(whole_kernel, out_shape=(S((1024, 256), bf), S((1024, 256)...  132 us
    pallas_call x1, Pallas kernels, attention(): pl.pallas_call(attention_kernel, out_shape=jax.ShapeDtypeStruct((1024, 25...  5.2 us

profile of v7, /device:TPU:0, one launch (start us, length us, event | category | flops | bytes accessed | tf_op | source)
XLA Modules:
  0.0 137.0 jit_solution(1647024799633234743)
XLA Ops:
  0.0 131.7 %whole.1 = (bf16[1024,256]{1,0:T(8,128)(2,1)}, bf16[1024,256]{1,0:T(8,128)(2,1)}) custom-call(bf16[128,1280]{1,0:T(8,128)(2,1)} %patches.1, s32[1,128]{1,0:T(1,128)} %ids.1, s32[1,32]{1,0:T(1,128)} %bitcast.11, s32[1,64]{1,0:T(1,128)} %slots.1, bf16[64,8192]{1,0:T(8,128)(2,1)} %text.1, f32[1280]{0:T(1024)} %vnorm.1, bf16[1280,1920]{1,0:T(8,128)(2,1)} %qkv_w.1, ...), custom_call_target="tpu_custom_call" | custom-call | tf_op jit(solution)/shard_map/whole/pallas_call | solution.py:565
  131.7 5.2 %attention.1 = bf16[1024,256]{1,0:T(8,128)(2,1)} custom-call(bf16[1024,256]{1,0:T(8,128)(2,1)} %get-tuple-element.7.q, bf16[1024,256]{1,0:T(8,128)(2,1)} %get-tuple-element.8.kv), custom_call_target="tpu_custom_call" | custom-call | tf_op jit(solution)/shard_map/attention/pallas_call | solution.py:647
